TPU v7x, 128 devices: a whole 4x4x4 slice. The times are simulated.
128 devices in a mesh: lat: 4 (over z), lon: 4 (over x_lo, core), lev: 8 (over y, x_hi).
Axes of the slice: x: 4 (x_hi: 2, x_lo: 2; x = x_hi * 2 + x_lo), y: 4, z: 4, core: 2. Of those that a mesh axis runs over, the one named last changes fastest.
Arguments:
- field_now: float32 [16, 256, 512, 128], P('lat', 'lon', 'lev'), may hold values from 0.2 to 1.8
- earlier: float32 [16, 256, 512, 128], P('lat', 'lon', 'lev'), may hold values from 0.2 to 1.8
- speed_square: float32 [16, 256, 512, 128], P('lat', 'lon', 'lev'), may hold values from 0.05 to 0.3
Outputs:
- field_now_end: float32 [16, 256, 512, 128], P('lat', 'lon', 'lev')
All inputs are finite; a program needn't handle non-finite values.
Results may differ from a plain program's by a relative error of at most 0.00002.
Values sent between devices are 32-bit elements; how exact they have to be, the bound alone decides.
A program may use at most 320 MiB of HBM per device.

v0:
```python
import jax
import jax.numpy as jnp
from jax import lax
from jax.sharding import PartitionSpec as P

STEPS = 4


def with_halo(value, sides, width):
    edges = {}
    for axis, dim in sides:
        peers, length = (lax.axis_size(axis), value.shape[dim])
        up = [(i, (i + 1) % peers) for i in range(peers - 1)]
        last = lax.slice_in_dim(value, length - width, length, axis=dim)
        initial = lax.slice_in_dim(value, 0, width, axis=dim)
        edges[dim] = (
            lax.ppermute(last, axis, up),
            lax.ppermute(initial, axis, [(b, a) for a, b in up]),
        )
    done = []
    for _, dim in sides:
        low, high = edges[dim]
        around = [(width, width) if d in done else (0, 0) for d in range(value.ndim)]
        value = jnp.concatenate([jnp.pad(low, around), value, jnp.pad(high, around)], axis=dim)
        done.append(dim)
    return value


def without_rim(values, dims):
    for dim in dims:
        values = lax.slice_in_dim(values, 1, values.shape[dim] - 1, axis=dim)
    return values


def shifted_cells(values, dim, start, dims):
    others = [other for other in dims if other != dim]
    values = without_rim(values, others)
    return lax.slice_in_dim(values, start, start + values.shape[dim] - 2, axis=dim)


def march_step(padded, before, speed_square):
    middle = without_rim(padded, (0, 1, 2))
    lower = [shifted_cells(padded, dim, 0, (0, 1, 2)) for dim in (0, 1, 2)]
    upper = [shifted_cells(padded, dim, 2, (0, 1, 2)) for dim in (0, 1, 2)]
    spread = lower[0] + upper[0] + lower[1] + upper[1] + lower[2] + upper[2] - 6.0 * middle
    return 2.0 * middle - before + speed_square * spread


def local(field_now, earlier, speed_square):
    for step in range(STEPS):
        padded = with_halo(field_now, (("lat", 0), ("lon", 1), ("lev", 2)), 1)
        later = march_step(padded, earlier, speed_square)
        earlier, field_now = (field_now, later)
    return field_now


def solution(mesh):
    return jax.shard_map(
        local,
        mesh=mesh,
        in_specs=(
            P("lat", "lon", "lev", None),
            P("lat", "lon", "lev", None),
            P("lat", "lon", "lev", None),
        ),
        out_specs=P("lat", "lon", "lev", None),
        check_vma=False,
    )
```

profile of v0, /device:TPU:1, one launch (start us, length us, event | category | flops | bytes accessed | tf_op | source)
XLA Modules:
  0.0 331.0 jit_solution(494516340778882127)
XLA Ops:
  0.0 4.1 %fusion.51 = (f32[1,64,64,128]{3,2,1,0:T(8,128)}, f32[1,64,64,128]{3,2,1,0:T(8,128)S(1)}) fusion(f32[4,64,64,128]{3,2,1,0:T(8,128)} %param.3), kind=kLoop, calls=%fused_computation.120 | loop fusion | bytes 8388608 | tf_op jit(solution)/shard_map/slice | solution.py:15
  4.1 4.6 %collective-permute-start = (f32[1,64,64,128]{3,2,1,0:T(8,128)S(1)}, f32[1,64,64,128]{3,2,1,0:T(8,128)S(1)}, u32[]{:S(2)}, u32[]{:S(2)}) collective-permute-start(f32[1,64,64,128]{3,2,1,0:T(8,128)S(1)} %get-tuple-element.28), channel_id=1, source_target_pairs={{0,32},{32,64},{64,96},{1,33},{33,65},{65,97},{2,34},{34,66},{66,9... | collective-permute-start | bytes 6291464 | tf_op jit(solution)/shard_map/ppermute | solution.py:17
  16.2 4.4 %collective-permute-start.4 = (f32[4,64,1,128]{3,1,2,0:T(8,128)S(1)}, f32[4,64,1,128]{3,1,2,0:T(8,128)S(1)}, u32[]{:S(2)}, u32[]{:S(2)}) collective-permute-start(f32[4,64,1,128]{3,1,2,0:T(8,128)S(1)} %bitcast.27), channel_id=1, source_target_pairs={{0,1},{1,2},{2,3},{3,4},{4,5},{5,6},{6,7},{8,9},{9,10},{10,11},{11... | collective-permute-start | bytes 393224 | tf_op jit(solution)/shard_map/ppermute | solution.py:17
  21.9 31.0 %collective-permute-done = f32[1,64,64,128]{3,2,1,0:T(8,128)S(1)} collective-permute-done((f32[1,64,64,128]{3,2,1,0:T(8,128)S(1)}, f32[1,64,64,128]{3,2,1,0:T(8,128)S(1)}, u32[]{:S(2)}, u32[]{:S(2)}) %collective-permute-start) | collective-permute-done | bytes 2097184 | tf_op jit(solution)/shard_map/ppermute | solution.py:17
  54.4 4.7 %constant_dynamic-update-slice_fusion.1 = f32[6,64,64,128]{3,2,1,0:T(8,128)} fusion(f32[6,64,64,128]{3,2,1,0:T(8,128)} %constant_dynamic-update-slice_fusion.2, f32[4,64,64,128]{3,2,1,0:T(8,128)S(1)} %copy-done), kind=kLoop, calls=%fused_computation.107 | loop fusion | bytes 16777216
  61.9 26.1 %fusion.34 = f32[4,64,64,128]{3,2,1,0:T(8,128)} fusion(f32[4,64,64,128]{3,2,1,0:T(8,128)S(1)} %bitcast.17, f32[4,64,1,128]{3,2,1,0:T(1,128)S(1)} %bitcast.22, f32[6,1,64,128]{3,2,1,0:T(8,128)S(1)} %pad.51, f32[6,64,64,128]{3,2,1,0:T(8,128)} %constant_dynamic-update-slice_fusion, f32[6,1,64,128]{3,2,1,0:T(8,128)S(1)} %pad.50, ...), kind=kLoop, calls=%fused_computation.89 | loop fusion | flops 56623104 | bytes 50987008 | tf_op jit(solution)/shard_map/add | solution.py:46
  90.6 4.2 %collective-permute-start.6 = (f32[1,64,64,128]{3,2,1,0:T(8,128)S(1)}, f32[1,64,64,128]{3,2,1,0:T(8,128)S(1)}, u32[]{:S(2)}, u32[]{:S(2)}) collective-permute-start(f32[1,64,64,128]{3,2,1,0:T(8,128)S(1)} %get-tuple-element.19), channel_id=1, source_target_pairs={{0,32},{32,64},{64,96},{1,33},{33,65},{65,97},{2,34},{34,66},{66,9... | collective-permute-start | bytes 6291464 | tf_op jit(solution)/shard_map/ppermute | solution.py:17
  97.1 4.8 %collective-permute-start.8 = (f32[4,1,64,128]{3,2,1,0:T(8,128)S(1)}, f32[4,1,64,128]{3,2,1,0:T(8,128)S(1)}, u32[]{:S(2)}, u32[]{:S(2)}) collective-permute-start(f32[4,1,64,128]{3,2,1,0:T(8,128)S(1)} %get-tuple-element.21), channel_id=1, source_target_pairs={{0,8},{8,16},{16,24},{1,9},{9,17},{17,25},{2,10},{10,18},{18,26},{... | collective-permute-start | bytes 393224 | tf_op jit(solution)/shard_map/ppermute | solution.py:17
  105.6 4.4 %collective-permute-start.10 = (f32[4,64,1,128]{3,1,2,0:T(8,128)S(1)}, f32[4,64,1,128]{3,1,2,0:T(8,128)S(1)}, u32[]{:S(2)}, u32[]{:S(2)}) collective-permute-start(f32[4,64,1,128]{3,1,2,0:T(8,128)S(1)} %bitcast.32), channel_id=1, source_target_pairs={{0,1},{1,2},{2,3},{3,4},{4,5},{5,6},{6,7},{8,9},{9,10},{10,11},{11... | collective-permute-start | bytes 393224 | tf_op jit(solution)/shard_map/ppermute | solution.py:17
  111.9 5.4 %collective-permute-done.11 = f32[4,64,1,128]{3,1,2,0:T(8,128)S(1)} collective-permute-done((f32[4,64,1,128]{3,1,2,0:T(8,128)S(1)}, f32[4,64,1,128]{3,1,2,0:T(8,128)S(1)}, u32[]{:S(2)}, u32[]{:S(2)}) %collective-permute-start.11) | collective-permute-done | bytes 131104 | tf_op jit(solution)/shard_map/ppermute | solution.py:18
  117.3 20.8 %collective-permute-done.6 = f32[1,64,64,128]{3,2,1,0:T(8,128)S(1)} collective-permute-done((f32[1,64,64,128]{3,2,1,0:T(8,128)S(1)}, f32[1,64,64,128]{3,2,1,0:T(8,128)S(1)}, u32[]{:S(2)}, u32[]{:S(2)}) %collective-permute-start.6) | collective-permute-done | bytes 2097184 | tf_op jit(solution)/shard_map/ppermute | solution.py:17
  138.1 4.2 %collective-permute-done.7 = f32[1,64,64,128]{3,2,1,0:T(8,128)} collective-permute-done((f32[1,64,64,128]{3,2,1,0:T(8,128)S(1)}, f32[1,64,64,128]{3,2,1,0:T(8,128)}, u32[]{:S(2)}, u32[]{:S(2)}) %collective-permute-start.7) | collective-permute-done | bytes 2097184 | tf_op jit(solution)/shard_map/ppermute | solution.py:18
  142.3 28.5 %fusion.24 = f32[4,64,64,128]{3,2,1,0:T(8,128)} fusion(f32[4,64,64,128]{3,2,1,0:T(8,128)} %param.5, f32[4,64,1,128]{3,2,1,0:T(1,128)S(1)} %bitcast.25, f32[6,1,64,128]{3,2,1,0:T(8,128)S(1)} %pad.55, f32[6,1,64,128]{3,2,1,0:T(8,128)S(1)} %pad.54, f32[1,64,64,128]{3,2,1,0:T(8,128)} %collective-permute-done.7, f32[4,64,64,128]{3,2,1,0:T(8,128)} %fusion.34, ...), kind=kLoop, calls=%fused_computation.61 | loop fusion | flops 73400320 | bytes 38404096 | tf_op jit(solution)/shard_map/add | solution.py:46
  179.1 6.0 %collective-permute-start.14 = (f32[4,1,64,128]{3,2,1,0:T(8,128)S(1)}, f32[4,1,64,128]{3,2,1,0:T(8,128)S(1)}, u32[]{:S(2)}, u32[]{:S(2)}) collective-permute-start(f32[4,1,64,128]{3,2,1,0:T(8,128)S(1)} %get-tuple-element.15), channel_id=1, source_target_pairs={{0,8},{8,16},{16,24},{1,9},{9,17},{17,25},{2,10},{10,18},{18,26},{... | collective-permute-start | bytes 393224 | tf_op jit(solution)/shard_map/ppermute | solution.py:17
  188.8 4.4 %collective-permute-start.16 = (f32[4,64,1,128]{3,1,2,0:T(8,128)S(1)}, f32[4,64,1,128]{3,1,2,0:T(8,128)S(1)}, u32[]{:S(2)}, u32[]{:S(2)}) collective-permute-start(f32[4,64,1,128]{3,1,2,0:T(8,128)S(1)} %bitcast.33), channel_id=1, source_target_pairs={{0,1},{1,2},{2,3},{3,4},{4,5},{5,6},{6,7},{8,9},{9,10},{10,11},{11... | collective-permute-start | bytes 393224 | tf_op jit(solution)/shard_map/ppermute | solution.py:17
  195.1 5.4 %collective-permute-done.17 = f32[4,64,1,128]{3,1,2,0:T(8,128)S(1)} collective-permute-done((f32[4,64,1,128]{3,1,2,0:T(8,128)S(1)}, f32[4,64,1,128]{3,1,2,0:T(8,128)S(1)}, u32[]{:S(2)}, u32[]{:S(2)}) %collective-permute-start.17) | collective-permute-done | bytes 131104 | tf_op jit(solution)/shard_map/ppermute | solution.py:18
  200.5 18.5 %collective-permute-done.12 = f32[1,64,64,128]{3,2,1,0:T(8,128)S(1)} collective-permute-done((f32[1,64,64,128]{3,2,1,0:T(8,128)S(1)}, f32[1,64,64,128]{3,2,1,0:T(8,128)S(1)}, u32[]{:S(2)}, u32[]{:S(2)}) %collective-permute-start.12) | collective-permute-done | bytes 2097184 | tf_op jit(solution)/shard_map/ppermute | solution.py:17
  219.0 4.1 %collective-permute-done.13 = f32[1,64,64,128]{3,2,1,0:T(8,128)} collective-permute-done((f32[1,64,64,128]{3,2,1,0:T(8,128)S(1)}, f32[1,64,64,128]{3,2,1,0:T(8,128)}, u32[]{:S(2)}, u32[]{:S(2)}) %collective-permute-start.13) | collective-permute-done | bytes 2097184 | tf_op jit(solution)/shard_map/ppermute | solution.py:18
  223.1 28.5 %fusion.14 = f32[4,64,64,128]{3,2,1,0:T(8,128)} fusion(f32[4,64,64,128]{3,2,1,0:T(8,128)} %param.5, f32[4,64,1,128]{3,2,1,0:T(1,128)S(1)} %bitcast.24, f32[6,1,64,128]{3,2,1,0:T(8,128)S(1)} %pad.59, f32[6,1,64,128]{3,2,1,0:T(8,128)S(1)} %pad.58, f32[1,64,64,128]{3,2,1,0:T(8,128)} %collective-permute-done.13, f32[4,64,64,128]{3,2,1,0:T(8,128)} %fusion.24, ...), kind=kLoop, calls=%fused_computation.33 | loop fusion | flops 73400320 | bytes 38404096 | tf_op jit(solution)/shard_map/add | solution.py:46
  259.6 7.1 %collective-permute-start.20 = (f32[4,1,64,128]{3,2,1,0:T(8,128)S(1)}, f32[4,1,64,128]{3,2,1,0:T(8,128)S(1)}, u32[]{:S(2)}, u32[]{:S(2)}) collective-permute-start(f32[4,1,64,128]{3,2,1,0:T(8,128)S(1)} %get-tuple-element.9), channel_id=1, source_target_pairs={{0,8},{8,16},{16,24},{1,9},{9,17},{17,25},{2,10},{10,18},{18,26},{... | collective-permute-start | bytes 393224 | tf_op jit(solution)/shard_map/ppermute | solution.py:17
  271.7 5.5 %collective-permute-start.22 = (f32[4,64,1,128]{3,1,2,0:T(8,128)S(1)}, f32[4,64,1,128]{3,1,2,0:T(8,128)S(1)}, u32[]{:S(2)}, u32[]{:S(2)}) collective-permute-start(f32[4,64,1,128]{3,1,2,0:T(8,128)S(1)} %bitcast.28), channel_id=1, source_target_pairs={{0,1},{1,2},{2,3},{3,4},{4,5},{5,6},{6,7},{8,9},{9,10},{10,11},{11... | collective-permute-start | bytes 393224 | tf_op jit(solution)/shard_map/ppermute | solution.py:17
  279.2 19.2 %collective-permute-done.18 = f32[1,64,64,128]{3,2,1,0:T(8,128)S(1)} collective-permute-done((f32[1,64,64,128]{3,2,1,0:T(8,128)S(1)}, f32[1,64,64,128]{3,2,1,0:T(8,128)S(1)}, u32[]{:S(2)}, u32[]{:S(2)}) %collective-permute-start.18) | collective-permute-done | bytes 2097184 | tf_op jit(solution)/shard_map/ppermute | solution.py:17
  298.4 4.1 %collective-permute-done.19 = f32[1,64,64,128]{3,2,1,0:T(8,128)} collective-permute-done((f32[1,64,64,128]{3,2,1,0:T(8,128)S(1)}, f32[1,64,64,128]{3,2,1,0:T(8,128)}, u32[]{:S(2)}, u32[]{:S(2)}) %collective-permute-start.19) | collective-permute-done | bytes 2097184 | tf_op jit(solution)/shard_map/ppermute | solution.py:18
  302.5 28.4 %fusion.4 = f32[4,64,64,128]{3,2,1,0:T(8,128)} fusion(f32[4,64,64,128]{3,2,1,0:T(8,128)} %param.5, f32[4,64,1,128]{3,2,1,0:T(1,128)S(1)} %bitcast.19, f32[6,1,64,128]{3,2,1,0:T(8,128)S(1)} %pad.63, f32[6,1,64,128]{3,2,1,0:T(8,128)S(1)} %pad.62, f32[1,64,64,128]{3,2,1,0:T(8,128)} %collective-permute-done.19, f32[4,64,64,128]{3,2,1,0:T(8,128)} %fusion.14, ...), kind=kLoop, calls=%fused_computation.5 | loop fusion | flops 73400320 | bytes 38404096 | tf_op jit(solution)/shard_map/add | solution.py:46
  (60 shorter events, 52.1 us)
Async XLA Ops:
  4.1 48.8 %collective-permute-start = (f32[1,64,64,128]{3,2,1,0:T(8,128)S(1)}, f32[1,64,64,128]{3,2,1,0:T(8,128)S(1)}, u32[]{:S(2)}, u32[]{:S(2)}) collective-permute-start(f32[1,64,64,128]{3,2,1,0:T(8,128)S(1)} %get-tuple-element.28), channel_id=1, source_target_pairs={{0,32},{32,64},{64,96},{1,33},{33,65},{65,97},{2,34},{34,66},{66,9... | collective-permute-start | bytes 6291464 | tf_op jit(solution)/shard_map/ppermute | solution.py:17
  8.8 50.3 %collective-permute-start.1 = (f32[1,64,64,128]{3,2,1,0:T(8,128)}, f32[1,64,64,128]{3,2,1,0:T(8,128)S(1)}, u32[]{:S(2)}, u32[]{:S(2)}) collective-permute-start(f32[1,64,64,128]{3,2,1,0:T(8,128)} %get-tuple-element.27), channel_id=1, source_target_pairs={{32,0},{64,32},{96,64},{33,1},{65,33},{97,65},{34,2},{66,34},{98,6... | collective-permute-start | bytes 6291464 | tf_op jit(solution)/shard_map/ppermute | solution.py:18
  10.1 10.5 %collective-permute-start.2 = (f32[4,1,64,128]{3,2,1,0:T(8,128)S(1)}, f32[4,1,64,128]{3,2,1,0:T(8,128)S(1)}, u32[]{:S(2)}, u32[]{:S(2)}) collective-permute-start(f32[4,1,64,128]{3,2,1,0:T(8,128)S(1)} %get-tuple-element.25), channel_id=1, source_target_pairs={{0,8},{8,16},{16,24},{1,9},{9,17},{17,25},{2,10},{10,18},{18,26},{... | collective-permute-start | bytes 393224 | tf_op jit(solution)/shard_map/ppermute | solution.py:17
  14.1 7.8 %collective-permute-start.3 = (f32[4,1,64,128]{3,2,1,0:T(8,128)S(1)}, f32[4,1,64,128]{3,2,1,0:T(8,128)S(1)}, u32[]{:S(2)}, u32[]{:S(2)}) collective-permute-start(f32[4,1,64,128]{3,2,1,0:T(8,128)S(1)} %get-tuple-element.26), channel_id=1, source_target_pairs={{8,0},{16,8},{24,16},{9,1},{17,9},{25,17},{10,2},{18,10},{26,18},{... | collective-permute-start | bytes 393224 | tf_op jit(solution)/shard_map/ppermute | solution.py:18
  16.2 45.7 %collective-permute-start.4 = (f32[4,64,1,128]{3,1,2,0:T(8,128)S(1)}, f32[4,64,1,128]{3,1,2,0:T(8,128)S(1)}, u32[]{:S(2)}, u32[]{:S(2)}) collective-permute-start(f32[4,64,1,128]{3,1,2,0:T(8,128)S(1)} %bitcast.27), channel_id=1, source_target_pairs={{0,1},{1,2},{2,3},{3,4},{4,5},{5,6},{6,7},{8,9},{9,10},{10,11},{11... | collective-permute-start | bytes 393224 | tf_op jit(solution)/shard_map/ppermute | solution.py:17
  20.6 41.3 %collective-permute-start.5 = (f32[4,64,1,128]{3,1,2,0:T(8,128)S(1)}, f32[4,64,1,128]{3,1,2,0:T(8,128)S(1)}, u32[]{:S(2)}, u32[]{:S(2)}) collective-permute-start(f32[4,64,1,128]{3,1,2,0:T(8,128)S(1)} %bitcast.26), channel_id=1, source_target_pairs={{1,0},{2,1},{3,2},{4,3},{5,4},{6,5},{7,6},{9,8},{10,9},{11,10},{12... | collective-permute-start | bytes 393224 | tf_op jit(solution)/shard_map/ppermute | solution.py:18
  90.6 47.6 %collective-permute-start.6 = (f32[1,64,64,128]{3,2,1,0:T(8,128)S(1)}, f32[1,64,64,128]{3,2,1,0:T(8,128)S(1)}, u32[]{:S(2)}, u32[]{:S(2)}) collective-permute-start(f32[1,64,64,128]{3,2,1,0:T(8,128)S(1)} %get-tuple-element.19), channel_id=1, source_target_pairs={{0,32},{32,64},{64,96},{1,33},{33,65},{65,97},{2,34},{34,66},{66,9... | collective-permute-start | bytes 6291464 | tf_op jit(solution)/shard_map/ppermute | solution.py:17
  94.8 47.5 %collective-permute-start.7 = (f32[1,64,64,128]{3,2,1,0:T(8,128)S(1)}, f32[1,64,64,128]{3,2,1,0:T(8,128)}, u32[]{:S(2)}, u32[]{:S(2)}) collective-permute-start(f32[1,64,64,128]{3,2,1,0:T(8,128)S(1)} %get-tuple-element.20), channel_id=1, source_target_pairs={{32,0},{64,32},{96,64},{33,1},{65,33},{97,65},{34,2},{66,34},{98,6... | collective-permute-start | bytes 6291464 | tf_op jit(solution)/shard_map/ppermute | solution.py:18
  97.1 12.9 %collective-permute-start.8 = (f32[4,1,64,128]{3,2,1,0:T(8,128)S(1)}, f32[4,1,64,128]{3,2,1,0:T(8,128)S(1)}, u32[]{:S(2)}, u32[]{:S(2)}) collective-permute-start(f32[4,1,64,128]{3,2,1,0:T(8,128)S(1)} %get-tuple-element.21), channel_id=1, source_target_pairs={{0,8},{8,16},{16,24},{1,9},{9,17},{17,25},{2,10},{10,18},{18,26},{... | collective-permute-start | bytes 393224 | tf_op jit(solution)/shard_map/ppermute | solution.py:17
  101.9 9.4 %collective-permute-start.9 = (f32[4,1,64,128]{3,2,1,0:T(8,128)S(1)}, f32[4,1,64,128]{3,2,1,0:T(8,128)S(1)}, u32[]{:S(2)}, u32[]{:S(2)}) collective-permute-start(f32[4,1,64,128]{3,2,1,0:T(8,128)S(1)} %get-tuple-element.22), channel_id=1, source_target_pairs={{8,0},{16,8},{24,16},{9,1},{17,9},{25,17},{10,2},{18,10},{26,18},{... | collective-permute-start | bytes 393224 | tf_op jit(solution)/shard_map/ppermute | solution.py:18
  105.6 6.3 %collective-permute-start.10 = (f32[4,64,1,128]{3,1,2,0:T(8,128)S(1)}, f32[4,64,1,128]{3,1,2,0:T(8,128)S(1)}, u32[]{:S(2)}, u32[]{:S(2)}) collective-permute-start(f32[4,64,1,128]{3,1,2,0:T(8,128)S(1)} %bitcast.32), channel_id=1, source_target_pairs={{0,1},{1,2},{2,3},{3,4},{4,5},{5,6},{6,7},{8,9},{9,10},{10,11},{11... | collective-permute-start | bytes 393224 | tf_op jit(solution)/shard_map/ppermute | solution.py:17
  110.0 7.3 %collective-permute-start.11 = (f32[4,64,1,128]{3,1,2,0:T(8,128)S(1)}, f32[4,64,1,128]{3,1,2,0:T(8,128)S(1)}, u32[]{:S(2)}, u32[]{:S(2)}) collective-permute-start(f32[4,64,1,128]{3,1,2,0:T(8,128)S(1)} %bitcast.29), channel_id=1, source_target_pairs={{1,0},{2,1},{3,2},{4,3},{5,4},{6,5},{7,6},{9,8},{10,9},{11,10},{12... | collective-permute-start | bytes 393224 | tf_op jit(solution)/shard_map/ppermute | solution.py:18
  173.4 45.6 %collective-permute-start.12 = (f32[1,64,64,128]{3,2,1,0:T(8,128)S(1)}, f32[1,64,64,128]{3,2,1,0:T(8,128)S(1)}, u32[]{:S(2)}, u32[]{:S(2)}) collective-permute-start(f32[1,64,64,128]{3,2,1,0:T(8,128)S(1)} %get-tuple-element.13), channel_id=1, source_target_pairs={{0,32},{32,64},{64,96},{1,33},{33,65},{65,97},{2,34},{34,66},{66,9... | collective-permute-start | bytes 6291464 | tf_op jit(solution)/shard_map/ppermute | solution.py:17
  176.8 46.2 %collective-permute-start.13 = (f32[1,64,64,128]{3,2,1,0:T(8,128)S(1)}, f32[1,64,64,128]{3,2,1,0:T(8,128)}, u32[]{:S(2)}, u32[]{:S(2)}) collective-permute-start(f32[1,64,64,128]{3,2,1,0:T(8,128)S(1)} %get-tuple-element.14), channel_id=1, source_target_pairs={{32,0},{64,32},{96,64},{33,1},{65,33},{97,65},{34,2},{66,34},{98,6... | collective-permute-start | bytes 6291464 | tf_op jit(solution)/shard_map/ppermute | solution.py:18
  179.1 14.0 %collective-permute-start.14 = (f32[4,1,64,128]{3,2,1,0:T(8,128)S(1)}, f32[4,1,64,128]{3,2,1,0:T(8,128)S(1)}, u32[]{:S(2)}, u32[]{:S(2)}) collective-permute-start(f32[4,1,64,128]{3,2,1,0:T(8,128)S(1)} %get-tuple-element.15), channel_id=1, source_target_pairs={{0,8},{8,16},{16,24},{1,9},{9,17},{17,25},{2,10},{10,18},{18,26},{... | collective-permute-start | bytes 393224 | tf_op jit(solution)/shard_map/ppermute | solution.py:17
  185.1 9.6 %collective-permute-start.15 = (f32[4,1,64,128]{3,2,1,0:T(8,128)S(1)}, f32[4,1,64,128]{3,2,1,0:T(8,128)S(1)}, u32[]{:S(2)}, u32[]{:S(2)}) collective-permute-start(f32[4,1,64,128]{3,2,1,0:T(8,128)S(1)} %get-tuple-element.16), channel_id=1, source_target_pairs={{8,0},{16,8},{24,16},{9,1},{17,9},{25,17},{10,2},{18,10},{26,18},{... | collective-permute-start | bytes 393224 | tf_op jit(solution)/shard_map/ppermute | solution.py:18
  188.8 6.3 %collective-permute-start.16 = (f32[4,64,1,128]{3,1,2,0:T(8,128)S(1)}, f32[4,64,1,128]{3,1,2,0:T(8,128)S(1)}, u32[]{:S(2)}, u32[]{:S(2)}) collective-permute-start(f32[4,64,1,128]{3,1,2,0:T(8,128)S(1)} %bitcast.33), channel_id=1, source_target_pairs={{0,1},{1,2},{2,3},{3,4},{4,5},{5,6},{6,7},{8,9},{9,10},{10,11},{11... | collective-permute-start | bytes 393224 | tf_op jit(solution)/shard_map/ppermute | solution.py:17
  193.1 7.3 %collective-permute-start.17 = (f32[4,64,1,128]{3,1,2,0:T(8,128)S(1)}, f32[4,64,1,128]{3,1,2,0:T(8,128)S(1)}, u32[]{:S(2)}, u32[]{:S(2)}) collective-permute-start(f32[4,64,1,128]{3,1,2,0:T(8,128)S(1)} %bitcast.30), channel_id=1, source_target_pairs={{1,0},{2,1},{3,2},{4,3},{5,4},{6,5},{7,6},{9,8},{10,9},{11,10},{12... | collective-permute-start | bytes 393224 | tf_op jit(solution)/shard_map/ppermute | solution.py:18
  254.1 44.3 %collective-permute-start.18 = (f32[1,64,64,128]{3,2,1,0:T(8,128)S(1)}, f32[1,64,64,128]{3,2,1,0:T(8,128)S(1)}, u32[]{:S(2)}, u32[]{:S(2)}) collective-permute-start(f32[1,64,64,128]{3,2,1,0:T(8,128)S(1)} %get-tuple-element.7), channel_id=1, source_target_pairs={{0,32},{32,64},{64,96},{1,33},{33,65},{65,97},{2,34},{34,66},{66,9... | collective-permute-start | bytes 6291464 | tf_op jit(solution)/shard_map/ppermute | solution.py:17
  257.4 45.1 %collective-permute-start.19 = (f32[1,64,64,128]{3,2,1,0:T(8,128)S(1)}, f32[1,64,64,128]{3,2,1,0:T(8,128)}, u32[]{:S(2)}, u32[]{:S(2)}) collective-permute-start(f32[1,64,64,128]{3,2,1,0:T(8,128)S(1)} %get-tuple-element.8), channel_id=1, source_target_pairs={{32,0},{64,32},{96,64},{33,1},{65,33},{97,65},{34,2},{66,34},{98,6... | collective-permute-start | bytes 6291464 | tf_op jit(solution)/shard_map/ppermute | solution.py:18
  259.6 12.1 %collective-permute-start.20 = (f32[4,1,64,128]{3,2,1,0:T(8,128)S(1)}, f32[4,1,64,128]{3,2,1,0:T(8,128)S(1)}, u32[]{:S(2)}, u32[]{:S(2)}) collective-permute-start(f32[4,1,64,128]{3,2,1,0:T(8,128)S(1)} %get-tuple-element.9), channel_id=1, source_target_pairs={{0,8},{8,16},{16,24},{1,9},{9,17},{17,25},{2,10},{10,18},{18,26},{... | collective-permute-start | bytes 393224 | tf_op jit(solution)/shard_map/ppermute | solution.py:17
  266.7 10.5 %collective-permute-start.21 = (f32[4,1,64,128]{3,2,1,0:T(8,128)S(1)}, f32[4,1,64,128]{3,2,1,0:T(8,128)S(1)}, u32[]{:S(2)}, u32[]{:S(2)}) collective-permute-start(f32[4,1,64,128]{3,2,1,0:T(8,128)S(1)} %get-tuple-element.10), channel_id=1, source_target_pairs={{8,0},{16,8},{24,16},{9,1},{17,9},{25,17},{10,2},{18,10},{26,18},{... | collective-permute-start | bytes 393224 | tf_op jit(solution)/shard_map/ppermute | solution.py:18
  270.4 7.2 %collective-permute-start.23 = (f32[4,64,1,128]{3,1,2,0:T(8,128)S(1)}, f32[4,64,1,128]{3,1,2,0:T(8,128)S(1)}, u32[]{:S(2)}, u32[]{:S(2)}) collective-permute-start(f32[4,64,1,128]{3,1,2,0:T(8,128)S(1)} %bitcast.31), channel_id=1, source_target_pairs={{1,0},{2,1},{3,2},{4,3},{5,4},{6,5},{7,6},{9,8},{10,9},{11,10},{12... | collective-permute-start | bytes 393224 | tf_op jit(solution)/shard_map/ppermute | solution.py:18
  271.7 7.4 %collective-permute-start.22 = (f32[4,64,1,128]{3,1,2,0:T(8,128)S(1)}, f32[4,64,1,128]{3,1,2,0:T(8,128)S(1)}, u32[]{:S(2)}, u32[]{:S(2)}) collective-permute-start(f32[4,64,1,128]{3,1,2,0:T(8,128)S(1)} %bitcast.28), channel_id=1, source_target_pairs={{0,1},{1,2},{2,3},{3,4},{4,5},{5,6},{6,7},{8,9},{9,10},{10,11},{11... | collective-permute-start | bytes 393224 | tf_op jit(solution)/shard_map/ppermute | solution.py:17
  (4 other events, 27.9 us)
where the time goes:
time: 335 us; the launch traced here: 331 us
  waiting for transfers between devices  116 us (35%)
  other arithmetic  112 us (33%)
  starting transfers between devices  74.1 us (22%)
  local copies, waits for them, and re-layouts  29.3 us (9%)
    add x4, other arithmetic, march_step(): return 2.0 * middle - before + speed_square * spread  112 us
    ppermute x12, waiting for transfers between devices, with_halo(): lax.ppermute(last, axis, up)  92.1 us
    ppermute x12, starting transfers between devices, with_halo(): lax.ppermute(last, axis, up)  55.9 us
    ppermute x12, waiting for transfers between devices, with_halo(): lax.ppermute(initial, axis, [(b, a) for a, b in up])  23.5 us
    ppermute x12, starting transfers between devices, with_halo(): lax.ppermute(initial, axis, [(b, a) for a, b in up])  18.2 us
    slice x11, local copies, waits for them, and re-layouts, with_halo(): last = lax.slice_in_dim(value, length - width, length, axis=dim)  16 us
    unnamed x10, local copies, waits for them, and re-layouts  7.47 us
  transfers between devices with their start and end apart: 24, of which 13 were waited for; matrix products, arithmetic and copies ran while one was open for 5% of the time, Pallas kernels for 0%

commit v1 on v0

v1 whole, which is shorter than its diff:
```python
import functools

import jax
import jax.numpy as jnp
from jax import lax
from jax.experimental import pallas as pl
from jax.experimental.pallas import tpu as pltpu
from jax.sharding import PartitionSpec as P

STEPS = 4
CHUNK = 8
MESH = pl.DeviceIdType.MESH


def kernel(
    now_ref, earlier_ref, speed_ref, out_ref,
    field, speed, halo_j, halo_k, pack_k,
    load_sem, out_sem, send_j, recv_j, send_i, recv_i, send_k, recv_k,
):
    planes, rows, depth, _ = now_ref.shape
    chunks = rows // CHUNK
    place = [lax.axis_index(axis) for axis in ("lat", "lon", "lev")]
    sizes = [lax.axis_size(axis) for axis in ("lat", "lon", "lev")]
    has = [(at > 0, at < size - 1) for at, size in zip(place, sizes)]
    towards = [
        tuple({axis: at + shift} for shift in (-1, 1))
        for axis, at in zip(("lat", "lon", "lev"), place)
    ]

    loads = [
        pltpu.make_async_copy(now_ref, field.at[0, :, pl.ds(1, rows)], load_sem.at[0]),
        pltpu.make_async_copy(earlier_ref, field.at[1, :, pl.ds(1, rows)], load_sem.at[1]),
        pltpu.make_async_copy(speed_ref, speed, load_sem.at[2]),
    ]
    for load in loads:
        load.start()

    barrier = pltpu.get_barrier_semaphore()
    count = 0
    for axis in range(3):
        for side in range(2):
            count = count + has[axis][side].astype(jnp.int32)

            @pl.when(has[axis][side])
            def _():
                pl.semaphore_signal(barrier, inc=1, device_id=towards[axis][side], device_id_type=MESH)

    pl.semaphore_wait(barrier, count)

    def copy_j(step, chunk, side):
        plane = (planes - 1) * side
        at = pl.multiple_of(chunk * CHUNK, CHUNK)
        if step == 0:
            source = now_ref.at[plane, pl.ds(at, CHUNK)]
        else:
            source = field.at[step % 2, plane, pl.ds(at + 1, CHUNK)]
        return pltpu.make_async_remote_copy(
            src_ref=source,
            dst_ref=halo_j.at[step, 1 - side, pl.ds(at, CHUNK)],
            send_sem=send_j.at[step, side, chunk],
            recv_sem=recv_j.at[step, 1 - side, chunk],
            device_id=towards[0][side],
            device_id_type=MESH,
        )

    def wait_j(step, chunk, side):
        at = pl.multiple_of(chunk * CHUNK, CHUNK)
        piece = halo_j.at[step, side, pl.ds(at, CHUNK)]
        pltpu.make_async_remote_copy(
            src_ref=piece, dst_ref=piece,
            send_sem=send_j.at[step, 1 - side, chunk],
            recv_sem=recv_j.at[step, side, chunk],
            device_id=towards[0][side], device_id_type=MESH,
        ).wait_recv()

    def copy_i(step, side):
        return pltpu.make_async_remote_copy(
            src_ref=field.at[step % 2, :, 1 + (rows - 1) * side],
            dst_ref=field.at[step % 2, :, (rows + 1) * (1 - side)],
            send_sem=send_i.at[step, side],
            recv_sem=recv_i.at[step, 1 - side],
            device_id=towards[1][side],
            device_id_type=MESH,
        )

    def copy_k(step, side):
        return pltpu.make_async_remote_copy(
            src_ref=pack_k.at[step, side],
            dst_ref=halo_k.at[step, 1 - side],
            send_sem=send_k.at[step, side],
            recv_sem=recv_k.at[step, 1 - side],
            device_id=towards[2][side],
            device_id_type=MESH,
        )

    def pack(step):
        def row(i, _):
            for plane in range(planes):
                for side in range(2):
                    pack_k[step, side, plane, pl.ds(i, 1), :] = field[step % 2, plane, i + 1, pl.ds((depth - 1) * side, 1), :]
            return 0

        lax.fori_loop(0, rows, row, 0)

    def send_sides(step):
        for side in range(2):
            @pl.when(has[1][side])
            def _():
                copy_i(step, side).start()

        for side in range(2):
            @pl.when(has[2][side])
            def _():
                copy_k(step, side).start()

    def wait_sides(step):
        for side in range(2):
            @pl.when(has[1][1 - side])
            def _():
                copy_i(step, side).wait_recv()

            @pl.when(has[2][1 - side])
            def _():
                copy_k(step, side).wait_recv()

    def wait_sides_sent(step):
        for side in range(2):
            @pl.when(has[1][side])
            def _():
                copy_i(step, side).wait_send()

            @pl.when(has[2][side])
            def _():
                copy_k(step, side).wait_send()

    def send_chunk(step, chunk):
        for side in range(2):
            @pl.when(has[0][side])
            def _():
                copy_j(step, chunk, side).start()

    def wait_chunk_sent(step, chunk):
        for side in range(2):
            @pl.when(has[0][side])
            def _():
                copy_j(step, chunk, side).wait_send()

    def each_chunk(body):
        def one(chunk, _):
            body(chunk)
            return 0

        lax.fori_loop(0, chunks, one, 0)

    each_chunk(lambda chunk: send_chunk(0, chunk))

    for side in range(2):
        @pl.when(jnp.logical_not(has[1][side]))
        def _():
            for slot in range(2):
                field[slot, :, (rows + 1) * side] = jnp.zeros((planes, depth, 128), jnp.float32)

        @pl.when(jnp.logical_not(has[2][side]))
        def _():
            for step in range(STEPS):
                for plane in range(planes):
                    halo_k[step, side, plane] = jnp.zeros((rows, 128), jnp.float32)

        @pl.when(jnp.logical_not(has[0][side]))
        def _():
            def row(i, _):
                halo_j[0, side, i] = jnp.zeros((depth, 128), jnp.float32)
                return 0

            lax.fori_loop(0, rows, row, 0)

    loads[0].wait()
    pack(0)
    send_sides(0)
    loads[1].wait()
    loads[2].wait()

    level = lax.broadcasted_iota(jnp.int32, (depth, 128), 0)
    first, last = level == 0, level == depth - 1

    def compute_row(step, i):
        old, new = step % 2, (step + 1) % 2
        slots = [jnp.where(has[0][side], step, 0) for side in range(2)]
        for plane in range(planes):
            here = field[old, plane, i + 1]
            below = halo_j[slots[0], 0, i] if plane == 0 else field[old, plane - 1, i + 1]
            above = halo_j[slots[1], 1, i] if plane == planes - 1 else field[old, plane + 1, i + 1]
            spread = below + above + field[old, plane, i] + field[old, plane, i + 2]
            k_low = jnp.where(first, halo_k[step, 0, plane, pl.ds(i, 1), :], pltpu.roll(here, 1, 0))
            k_high = jnp.where(last, halo_k[step, 1, plane, pl.ds(i, 1), :], pltpu.roll(here, depth - 1, 0))
            spread = spread + k_low + k_high - 6.0 * here
            field[new, plane, i + 1] = 2.0 * here - field[new, plane, i + 1] + speed[plane, i] * spread

    def copy_out(chunk):
        at = pl.multiple_of(chunk * CHUNK, CHUNK)
        return pltpu.make_async_copy(
            field.at[STEPS % 2, :, pl.ds(at + 1, CHUNK)], out_ref.at[:, pl.ds(at, CHUNK)], out_sem.at[chunk]
        )

    for step in range(STEPS):
        wait_sides(step)
        if step > 0:
            wait_sides_sent(step - 1)

        def one_chunk(chunk):
            if step > 0:
                wait_chunk_sent(step - 1, chunk)
            for side in range(2):
                @pl.when(has[0][side])
                def _():
                    wait_j(step, chunk, side)

            def row(i, _):
                compute_row(step, chunk * CHUNK + i)
                return 0

            lax.fori_loop(0, CHUNK, row, 0)
            if step < STEPS - 1:
                @pl.when(chunk > 0)
                def _():
                    send_chunk(step + 1, chunk - 1)
            else:
                copy_out(chunk).start()

        each_chunk(one_chunk)
        if step < STEPS - 1:
            pack(step + 1)
            send_chunk(step + 1, chunks - 1)
            send_sides(step + 1)

    wait_sides_sent(STEPS - 1)
    each_chunk(lambda chunk: wait_chunk_sent(STEPS - 1, chunk))
    each_chunk(lambda chunk: copy_out(chunk).wait())


def local(field_now, earlier, speed_square):
    planes, rows, depth, members = field_now.shape
    chunks = rows // CHUNK
    f32 = jnp.float32
    any_spec = pl.BlockSpec(memory_space=pl.ANY)
    return pl.pallas_call(
        kernel,
        out_shape=jax.ShapeDtypeStruct(field_now.shape, f32),
        in_specs=[any_spec] * 3,
        out_specs=any_spec,
        scratch_shapes=[
            pltpu.VMEM((2, planes, rows + 2, depth, members), f32),
            pltpu.VMEM((planes, rows, depth, members), f32),
            pltpu.VMEM((STEPS, 2, rows, depth, members), f32),
            pltpu.VMEM((STEPS, 2, planes, rows, members), f32),
            pltpu.VMEM((STEPS, 2, planes, rows, members), f32),
            pltpu.SemaphoreType.DMA((3,)),
            pltpu.SemaphoreType.DMA((chunks,)),
            pltpu.SemaphoreType.DMA((STEPS, 2, chunks)),
            pltpu.SemaphoreType.DMA((STEPS, 2, chunks)),
            pltpu.SemaphoreType.DMA((STEPS, 2)),
            pltpu.SemaphoreType.DMA((STEPS, 2)),
            pltpu.SemaphoreType.DMA((STEPS, 2)),
            pltpu.SemaphoreType.DMA((STEPS, 2)),
        ],
        compiler_params=pltpu.CompilerParams(
            collective_id=0, has_side_effects=True, vmem_limit_bytes=60 * 2**20
        ),
    )(field_now, earlier, speed_square)


def solution(mesh):
    spec = P("lat", "lon", "lev", None)
    return jax.shard_map(local, mesh=mesh, in_specs=(spec,) * 3, out_specs=spec, check_vma=False)
```

time: 335 us -> 197 us (0.59); the launches traced: 331 us -> 197 us
  Pallas kernels: 0 us -> 188 us
  waiting for transfers between devices: 116 us -> 0 us
  other arithmetic: 112 us -> 0 us
  starting transfers between devices: 74.1 us -> 0 us
  local copies, waits for them, and re-layouts: 29.3 us -> 8.44 us
    pallas_call x0 -> x1, Pallas kernels: none -> 188 us  [local(): pl.pallas_call(kernel, out_shape=jax.ShapeDtypeStruct(field_now.shape, f3...]
    ppermute x24 -> x0, waiting for transfers between devices: 116 us -> none  [the longest x12 92.1 us: with_halo(): lax.ppermute(last, axis, up)]
    add x4 -> x0, other arithmetic: 112 us -> none  [march_step(): return 2.0 * middle - before + speed_square * spread]
    ppermute x24 -> x0, starting transfers between devices: 74.1 us -> none  [the longest x12 55.9 us: with_halo(): lax.ppermute(last, axis, up)]
    slice x12 -> x0, local copies, waits for them, and re-layouts: 20.1 us -> none  [the longest x11 16 us: with_halo(): last = lax.slice_in_dim(value, length - width, length, axis=dim)]
    unnamed x10 -> x1, local copies, waits for them, and re-layouts: 7.47 us -> 8.44 us
  transfers between devices with their start and end apart: 24 -> 0, of which waited for: 13 -> 0; matrix products, arithmetic and copies ran while one was open for 5% -> 0% of each run, Pallas kernels for 0% -> 0%
where the time goes in v1:
time: 197 us
  Pallas kernels  188 us (95%)
  local copies, waits for them, and re-layouts  8.44 us (4%)
    pallas_call x1, Pallas kernels, local(): pl.pallas_call(kernel, out_shape=jax.ShapeDtypeStruct(field_now.shape, f3...  188 us
    unnamed x1, local copies, waits for them, and re-layouts  8.44 us

profile of v1, /device:TPU:1, one launch (start us, length us, event | category | flops | bytes accessed | tf_op | source)
XLA Modules:
  0.0 196.8 jit_solution(4447369240905209727)
XLA Ops:
  0.0 188.4 %shard_map.37 = f32[4,64,64,128]{3,2,1,0:T(8,128)} custom-call(f32[4,64,64,128]{3,2,1,0:T(8,128)} %now_ref.1, f32[4,64,64,128]{3,2,1,0:T(8,128)} %earlier_ref.1, f32[4,64,64,128]{3,2,1,0:T(8,128)} %speed_ref.1), custom_call_target="tpu_custom_call" | custom-call | tf_op jit(solution)/shard_map/pallas_call | solution.py:246
  188.4 8.4 %copy.5 = f32[4,64,64,128]{3,2,1,0:T(8,128)} copy(f32[4,64,64,128]{3,2,1,0:T(8,128)} %shard_map.37) | data formatting | bytes 16777216

commit v2 on v1

v2 whole, which is shorter than its diff:
```python
import functools

import jax
import jax.numpy as jnp
from jax import lax
from jax.experimental import pallas as pl
from jax.experimental.pallas import tpu as pltpu
from jax.sharding import PartitionSpec as P

STEPS = 4
CHUNK = 8
PIECE = (8, 8, 8, 4)
MESH = pl.DeviceIdType.MESH


def kernel(
    now_ref, earlier_ref, speed_ref, out_ref,
    field, speed, halo_j, halo_k, pack_k,
    load_sem, send_j, recv_j, send_i, recv_i, send_k, recv_k,
):
    planes, rows, depth, _ = now_ref.shape
    chunks = rows // CHUNK
    place = [lax.axis_index(axis) for axis in ("lat", "lon", "lev")]
    sizes = [lax.axis_size(axis) for axis in ("lat", "lon", "lev")]
    has = [(at > 0, at < size - 1) for at, size in zip(place, sizes)]
    towards = [
        tuple({axis: at + shift} for shift in (-1, 1))
        for axis, at in zip(("lat", "lon", "lev"), place)
    ]

    spans = [(plane, 1, at, size) for at, size in ((0, CHUNK), (CHUNK, rows - CHUNK)) for plane in (0, planes - 1)]
    spans.append((1, planes - 2, 0, rows))
    loads = [
        pltpu.make_async_copy(
            now_ref.at[pl.ds(plane, count), pl.ds(at, size)],
            field.at[0, pl.ds(plane, count), pl.ds(at + 1, size)],
            load_sem.at[index],
        )
        for index, (plane, count, at, size) in enumerate(spans)
    ]
    loads.append(pltpu.make_async_copy(earlier_ref, field.at[1, :, pl.ds(1, rows)], load_sem.at[5]))
    loads.append(pltpu.make_async_copy(speed_ref, speed, load_sem.at[6]))
    for load in loads:
        load.start()

    barrier = pltpu.get_barrier_semaphore()
    count = 0
    for axis in range(3):
        for side in range(2):
            count = count + has[axis][side].astype(jnp.int32)

            @pl.when(has[axis][side])
            def _():
                pl.semaphore_signal(barrier, inc=1, device_id=towards[axis][side], device_id_type=MESH)

    pl.semaphore_wait(barrier, count)

    def copy_j(step, piece, side):
        at = pl.multiple_of(piece * PIECE[step], PIECE[step])
        return pltpu.make_async_remote_copy(
            src_ref=field.at[step % 2, (planes - 1) * side, pl.ds(at + 1, PIECE[step])],
            dst_ref=halo_j.at[step, 1 - side, pl.ds(at, PIECE[step])],
            send_sem=send_j.at[step, side, piece],
            recv_sem=recv_j.at[step, 1 - side, piece],
            device_id=towards[0][side],
            device_id_type=MESH,
        )

    def copy_i(step, side):
        return pltpu.make_async_remote_copy(
            src_ref=field.at[step % 2, :, 1 + (rows - 1) * side],
            dst_ref=field.at[step % 2, :, (rows + 1) * (1 - side)],
            send_sem=send_i.at[step, side],
            recv_sem=recv_i.at[step, 1 - side],
            device_id=towards[1][side],
            device_id_type=MESH,
        )

    def copy_k(step, side):
        return pltpu.make_async_remote_copy(
            src_ref=pack_k.at[step, side],
            dst_ref=halo_k.at[step, 1 - side],
            send_sem=send_k.at[step, side],
            recv_sem=recv_k.at[step, 1 - side],
            device_id=towards[2][side],
            device_id_type=MESH,
        )

    def pack(step):
        def row(i, _):
            for plane in range(planes):
                for side in range(2):
                    pack_k[step, side, plane, pl.ds(i, 1), :] = field[step % 2, plane, i + 1, pl.ds((depth - 1) * side, 1), :]
            return 0

        lax.fori_loop(0, rows, row, 0)

    def send_sides(step):
        for side in range(2):
            @pl.when(has[1][side])
            def _():
                copy_i(step, side).start()

        for side in range(2):
            @pl.when(has[2][side])
            def _():
                copy_k(step, side).start()

    def wait_sides(step):
        for side in range(2):
            @pl.when(has[1][1 - side])
            def _():
                copy_i(step, side).wait_recv()

            @pl.when(has[2][1 - side])
            def _():
                copy_k(step, side).wait_recv()

    def wait_sides_sent(step):
        for side in range(2):
            @pl.when(has[1][side])
            def _():
                copy_i(step, side).wait_send()

            @pl.when(has[2][side])
            def _():
                copy_k(step, side).wait_send()

    def send_piece(step, piece):
        for side in range(2):
            @pl.when(has[0][side])
            def _():
                copy_j(step, piece, side).start()

    def wait_piece_sent(step, piece):
        for side in range(2):
            @pl.when(has[0][side])
            def _():
                copy_j(step, piece, side).wait_send()

    def wait_piece(step, piece):
        for side in range(2):
            @pl.when(has[0][1 - side])
            def _():
                copy_j(step, piece, side).wait_recv()

    def each(count, body):
        def one(index, _):
            body(index)
            return 0

        lax.fori_loop(0, count, one, 0)

    def send_chunk(step, chunk):
        pieces = CHUNK // PIECE[step]
        for index in range(pieces):
            send_piece(step, chunk * pieces + index)

    loads[0].wait()
    loads[1].wait()
    send_chunk(0, 0)
    loads[2].wait()
    loads[3].wait()
    each(chunks - 1, lambda chunk: send_chunk(0, chunk + 1))

    for side in range(2):
        @pl.when(jnp.logical_not(has[1][side]))
        def _():
            for slot in range(2):
                field[slot, :, (rows + 1) * side] = jnp.zeros((planes, depth, 128), jnp.float32)

        @pl.when(jnp.logical_not(has[2][side]))
        def _():
            for step in range(STEPS):
                for plane in range(planes):
                    halo_k[step, side, plane] = jnp.zeros((rows, 128), jnp.float32)

        @pl.when(jnp.logical_not(has[0][side]))
        def _():
            def row(i, _):
                halo_j[0, side, i] = jnp.zeros((depth, 128), jnp.float32)
                return 0

            lax.fori_loop(0, rows, row, 0)

    loads[4].wait()
    pack(0)
    send_sides(0)
    loads[5].wait()
    loads[6].wait()

    level = lax.broadcasted_iota(jnp.int32, (depth, 128), 0)
    first, last = level == 0, level == depth - 1

    def compute_row(step, i, some):
        old, new = step % 2, (step + 1) % 2
        slots = [jnp.where(has[0][side], step, 0) for side in range(2)]
        for plane in some:
            here = field[old, plane, i + 1]
            below = halo_j[slots[0], 0, i] if plane == 0 else field[old, plane - 1, i + 1]
            above = halo_j[slots[1], 1, i] if plane == planes - 1 else field[old, plane + 1, i + 1]
            spread = below + above + field[old, plane, i] + field[old, plane, i + 2]
            k_low = jnp.where(first, halo_k[step, 0, plane, pl.ds(i, 1), :], pltpu.roll(here, 1, 0))
            k_high = jnp.where(last, halo_k[step, 1, plane, pl.ds(i, 1), :], pltpu.roll(here, depth - 1, 0))
            spread = spread + k_low + k_high - 6.0 * here
            later = 2.0 * here - field[new, plane, i + 1] + speed[plane, i] * spread
            if step < STEPS - 1:
                field[new, plane, i + 1] = later
            else:
                out_ref[plane, i] = later

    def compute(step, at, size, some):
        each(size, lambda i: compute_row(step, at + i, some))

    for step in range(STEPS - 1):
        wait_sides(step)
        if step > 0:
            wait_sides_sent(step - 1)

        def one_chunk(chunk):
            if step > 0:
                wait_piece_sent(step - 1, chunk)
            wait_piece(step, chunk)
            compute(step, chunk * CHUNK, CHUNK, range(planes))

            @pl.when(chunk > 0)
            def _():
                send_chunk(step + 1, chunk - 1)

        each(chunks, one_chunk)
        pack(step + 1)
        send_chunk(step + 1, chunks - 1)
        send_sides(step + 1)

    last_step, size = STEPS - 1, PIECE[STEPS - 1]
    wait_sides(last_step)
    wait_sides_sent(last_step - 1)

    def one_piece(piece):
        compute(last_step, piece * size, size, range(1, planes - 1))
        wait_piece(last_step, piece)
        compute(last_step, piece * size, size, (0, planes - 1))

    each(rows // size, one_piece)
    each(chunks, lambda chunk: wait_piece_sent(last_step - 1, chunk))
    each(rows // size, lambda piece: wait_piece_sent(last_step, piece))
    wait_sides_sent(last_step)


def write_out(value_ref, out_ref, sem):
    rows = value_ref.shape[1]
    copies = [
        pltpu.make_async_copy(value_ref.at[:, pl.ds(at, CHUNK)], out_ref.at[:, pl.ds(at, CHUNK)], sem.at[at // CHUNK])
        for at in range(0, rows, CHUNK)
    ]
    for copy in copies:
        copy.start()
    for copy in copies:
        copy.wait()


def local(field_now, earlier, speed_square):
    planes, rows, depth, members = field_now.shape
    f32 = jnp.float32
    any_spec = pl.BlockSpec(memory_space=pl.ANY)
    later = pl.pallas_call(
        kernel,
        out_shape=pltpu.VMEM(field_now.shape, f32),
        in_specs=[any_spec] * 3,
        out_specs=pl.BlockSpec(memory_space=pltpu.VMEM),
        scratch_shapes=[
            pltpu.VMEM((2, planes, rows + 2, depth, members), f32),
            pltpu.VMEM((planes, rows, depth, members), f32),
            pltpu.VMEM((STEPS, 2, rows, depth, members), f32),
            pltpu.VMEM((STEPS, 2, planes, rows, members), f32),
            pltpu.VMEM((STEPS, 2, planes, rows, members), f32),
            pltpu.SemaphoreType.DMA((7,)),
            pltpu.SemaphoreType.DMA((STEPS, 2, rows // min(PIECE))),
            pltpu.SemaphoreType.DMA((STEPS, 2, rows // min(PIECE))),
            pltpu.SemaphoreType.DMA((STEPS, 2)),
            pltpu.SemaphoreType.DMA((STEPS, 2)),
            pltpu.SemaphoreType.DMA((STEPS, 2)),
            pltpu.SemaphoreType.DMA((STEPS, 2)),
        ],
        compiler_params=pltpu.CompilerParams(
            collective_id=0, has_side_effects=True, vmem_limit_bytes=46 * 2**20
        ),
    )(field_now, earlier, speed_square)
    return pl.pallas_call(
        write_out,
        out_shape=jax.ShapeDtypeStruct(field_now.shape, f32),
        in_specs=[pl.BlockSpec(memory_space=pltpu.VMEM)],
        out_specs=any_spec,
        scratch_shapes=[pltpu.SemaphoreType.DMA((rows // CHUNK,))],
        compiler_params=pltpu.CompilerParams(vmem_limit_bytes=2**20),
    )(later)


def solution(mesh):
    spec = P("lat", "lon", "lev", None)
    return jax.shard_map(local, mesh=mesh, in_specs=(spec,) * 3, out_specs=spec, check_vma=False)
```

time: 197 us -> 192 us (0.975)
  local copies, waits for them, and re-layouts: 8.44 us -> 0 us
  Pallas kernels: 188 us -> 191 us
    unnamed x1 -> x0, local copies, waits for them, and re-layouts: 8.44 us -> none
    pallas_call x1 -> x2, Pallas kernels: 188 us -> 191 us  [the longest x1 188 us: local(): pl.pallas_call(kernel, out_shape=pltpu.VMEM(field_now.shape, f32), in_spe...]
where the time goes in v2:
time: 192 us; the launch traced here: 191 us
  Pallas kernels  191 us (99%)
    pallas_call x1, Pallas kernels, local(): pl.pallas_call(kernel, out_shape=pltpu.VMEM(field_now.shape, f32), in_spe...  188 us

profile of v2, /device:TPU:1, one launch (start us, length us, event | category | flops | bytes accessed | tf_op | source)
XLA Modules:
  0.0 191.5 jit_solution(3918828757985270726)
XLA Ops:
  0.0 188.1 %shard_map.37.value_ref = f32[4,64,64,128]{3,2,1,0:T(8,128)S(1)} custom-call(f32[4,64,64,128]{3,2,1,0:T(8,128)} %now_ref.1, f32[4,64,64,128]{3,2,1,0:T(8,128)} %earlier_ref.1, f32[4,64,64,128]{3,2,1,0:T(8,128)} %speed_ref.1), custom_call_target="tpu_custom_call" | custom-call | tf_op jit(solution)/shard_map/pallas_call | solution.py:266
  188.1 3.4 %shard_map.38 = f32[4,64,64,128]{3,2,1,0:T(8,128)} custom-call(f32[4,64,64,128]{3,2,1,0:T(8,128)S(1)} %shard_map.37.value_ref), custom_call_target="tpu_custom_call" | custom-call | tf_op jit(solution)/shard_map/pallas_call | solution.py:289

commit v3 on v2

--- a/solution.py
+++ b/solution.py
@@ -8,9 +8,14 @@
 from jax.sharding import PartitionSpec as P
 
 STEPS = 4
-CHUNK = 8
-PIECE = (8, 8, 8, 4)
+PIECES = ((32, 32), (32, 32), (32, 32), (32, 24, 8))
+OUT = 8
 MESH = pl.DeviceIdType.MESH
+
+
+def cuts(step, rows):
+    sizes = [size * rows // sum(PIECES[step]) for size in PIECES[step]]
+    return [(sum(sizes[:index]), size) for index, size in enumerate(sizes)]
 
 
 def kernel(
@@ -19,7 +24,7 @@
     load_sem, send_j, recv_j, send_i, recv_i, send_k, recv_k,
 ):
     planes, rows, depth, _ = now_ref.shape
-    chunks = rows // CHUNK
+    pieces = [cuts(step, rows) for step in range(STEPS)]
     place = [lax.axis_index(axis) for axis in ("lat", "lon", "lev")]
     sizes = [lax.axis_size(axis) for axis in ("lat", "lon", "lev")]
     has = [(at > 0, at < size - 1) for at, size in zip(place, sizes)]
@@ -28,7 +33,7 @@
         for axis, at in zip(("lat", "lon", "lev"), place)
     ]
 
-    spans = [(plane, 1, at, size) for at, size in ((0, CHUNK), (CHUNK, rows - CHUNK)) for plane in (0, planes - 1)]
+    spans = [(plane, 1, at, size) for at, size in pieces[0] for plane in (0, planes - 1)]
     spans.append((1, planes - 2, 0, rows))
     loads = [
         pltpu.make_async_copy(
@@ -56,10 +61,10 @@
     pl.semaphore_wait(barrier, count)
 
     def copy_j(step, piece, side):
-        at = pl.multiple_of(piece * PIECE[step], PIECE[step])
+        at, size = pieces[step][piece]
         return pltpu.make_async_remote_copy(
-            src_ref=field.at[step % 2, (planes - 1) * side, pl.ds(at + 1, PIECE[step])],
-            dst_ref=halo_j.at[step, 1 - side, pl.ds(at, PIECE[step])],
+            src_ref=field.at[step % 2, (planes - 1) * side, pl.ds(at + 1, size)],
+            dst_ref=halo_j.at[step, 1 - side, pl.ds(at, size)],
             send_sem=send_j.at[step, side, piece],
             recv_sem=recv_j.at[step, 1 - side, piece],
             device_id=towards[0][side],
@@ -151,17 +156,10 @@
 
         lax.fori_loop(0, count, one, 0)
 
-    def send_chunk(step, chunk):
-        pieces = CHUNK // PIECE[step]
-        for index in range(pieces):
-            send_piece(step, chunk * pieces + index)
-
-    loads[0].wait()
-    loads[1].wait()
-    send_chunk(0, 0)
-    loads[2].wait()
-    loads[3].wait()
-    each(chunks - 1, lambda chunk: send_chunk(0, chunk + 1))
+    for piece in range(len(pieces[0])):
+        loads[2 * piece].wait()
+        loads[2 * piece + 1].wait()
+        send_piece(0, piece)
 
     for side in range(2):
         @pl.when(jnp.logical_not(has[1][side]))
@@ -216,42 +214,35 @@
         wait_sides(step)
         if step > 0:
             wait_sides_sent(step - 1)
-
-        def one_chunk(chunk):
+        sent = 0
+        for piece, (at, size) in enumerate(pieces[step]):
             if step > 0:
-                wait_piece_sent(step - 1, chunk)
-            wait_piece(step, chunk)
-            compute(step, chunk * CHUNK, CHUNK, range(planes))
-
-            @pl.when(chunk > 0)
-            def _():
-                send_chunk(step + 1, chunk - 1)
-
-        each(chunks, one_chunk)
+                wait_piece_sent(step - 1, piece)
+            wait_piece(step, piece)
+            compute(step, at, size, range(planes))
+            while sent < len(pieces[step + 1]) and sum(pieces[step + 1][sent]) <= at + size:
+                send_piece(step + 1, sent)
+                sent += 1
         pack(step + 1)
-        send_chunk(step + 1, chunks - 1)
         send_sides(step + 1)
 
-    last_step, size = STEPS - 1, PIECE[STEPS - 1]
-    wait_sides(last_step)
-    wait_sides_sent(last_step - 1)
-
-    def one_piece(piece):
-        compute(last_step, piece * size, size, range(1, planes - 1))
-        wait_piece(last_step, piece)
-        compute(last_step, piece * size, size, (0, planes - 1))
-
-    each(rows // size, one_piece)
-    each(chunks, lambda chunk: wait_piece_sent(last_step - 1, chunk))
-    each(rows // size, lambda piece: wait_piece_sent(last_step, piece))
-    wait_sides_sent(last_step)
+    step = STEPS - 1
+    wait_sides(step)
+    compute(step, 0, rows, range(1, planes - 1))
+    for piece, (at, size) in enumerate(pieces[step]):
+        wait_piece(step, piece)
+        compute(step, at, size, (0, planes - 1))
+    for before in (step - 1, step):
+        wait_sides_sent(before)
+        for piece in range(len(pieces[before])):
+            wait_piece_sent(before, piece)
 
 
 def write_out(value_ref, out_ref, sem):
     rows = value_ref.shape[1]
     copies = [
-        pltpu.make_async_copy(value_ref.at[:, pl.ds(at, CHUNK)], out_ref.at[:, pl.ds(at, CHUNK)], sem.at[at // CHUNK])
-        for at in range(0, rows, CHUNK)
+        pltpu.make_async_copy(value_ref.at[:, pl.ds(at, OUT)], out_ref.at[:, pl.ds(at, OUT)], sem.at[at // OUT])
+        for at in range(0, rows, OUT)
     ]
     for copy in copies:
         copy.start()
@@ -275,8 +266,8 @@
             pltpu.VMEM((STEPS, 2, planes, rows, members), f32),
             pltpu.VMEM((STEPS, 2, planes, rows, members), f32),
             pltpu.SemaphoreType.DMA((7,)),
-            pltpu.SemaphoreType.DMA((STEPS, 2, rows // min(PIECE))),
-            pltpu.SemaphoreType.DMA((STEPS, 2, rows // min(PIECE))),
+            pltpu.SemaphoreType.DMA((STEPS, 2, max(map(len, PIECES)))),
+            pltpu.SemaphoreType.DMA((STEPS, 2, max(map(len, PIECES)))),
             pltpu.SemaphoreType.DMA((STEPS, 2)),
             pltpu.SemaphoreType.DMA((STEPS, 2)),
             pltpu.SemaphoreType.DMA((STEPS, 2)),
@@ -291,7 +282,7 @@
         out_shape=jax.ShapeDtypeStruct(field_now.shape, f32),
         in_specs=[pl.BlockSpec(memory_space=pltpu.VMEM)],
         out_specs=any_spec,
-        scratch_shapes=[pltpu.SemaphoreType.DMA((rows // CHUNK,))],
+        scratch_shapes=[pltpu.SemaphoreType.DMA((rows // OUT,))],
         compiler_params=pltpu.CompilerParams(vmem_limit_bytes=2**20),
     )(later)
 

time: 192 us -> 190 us (0.990)
  no operation moved by 1% of the time
where the time goes in v3:
time: 190 us
  Pallas kernels  190 us (100%)
    pallas_call x1, Pallas kernels, local(): pl.pallas_call(kernel, out_shape=pltpu.VMEM(field_now.shape, f32), in_spe...  186 us

profile of v3, /device:TPU:1, one launch (start us, length us, event | category | flops | bytes accessed | tf_op | source)
XLA Modules:
  0.0 189.6 jit_solution(424176544727383006)
XLA Ops:
  0.0 186.2 %shard_map.37.value_ref = f32[4,64,64,128]{3,2,1,0:T(8,128)S(1)} custom-call(f32[4,64,64,128]{3,2,1,0:T(8,128)} %now_ref.1, f32[4,64,64,128]{3,2,1,0:T(8,128)} %earlier_ref.1, f32[4,64,64,128]{3,2,1,0:T(8,128)} %speed_ref.1), custom_call_target="tpu_custom_call" | custom-call | tf_op jit(solution)/shard_map/pallas_call | solution.py:257
  186.2 3.4 %shard_map.38 = f32[4,64,64,128]{3,2,1,0:T(8,128)} custom-call(f32[4,64,64,128]{3,2,1,0:T(8,128)S(1)} %shard_map.37.value_ref), custom_call_target="tpu_custom_call" | custom-call | tf_op jit(solution)/shard_map/pallas_call | solution.py:280

commit v4 on v3

--- a/solution.py
+++ b/solution.py
@@ -8,8 +8,8 @@
 from jax.sharding import PartitionSpec as P
 
 STEPS = 4
-PIECES = ((32, 32), (32, 32), (32, 32), (32, 24, 8))
-OUT = 8
+PIECES = ((32, 32), (32, 32), (32, 32), (28, 30, 6))
+EARLY = (1, 2)
 MESH = pl.DeviceIdType.MESH
 
 
@@ -19,12 +19,12 @@
 
 
 def kernel(
-    now_ref, earlier_ref, speed_ref, out_ref,
-    field, speed, halo_j, halo_k, pack_k,
+    now_ref, earlier_ref, speed_ref, inner_ref, outer_ref, face_ref, face_speed_ref, field, speed, halo_j, halo_k, pack_k,
     load_sem, send_j, recv_j, send_i, recv_i, send_k, recv_k,
 ):
     planes, rows, depth, _ = now_ref.shape
     pieces = [cuts(step, rows) for step in range(STEPS)]
+    begin = pieces[-1][min(EARLY)][0]
     place = [lax.axis_index(axis) for axis in ("lat", "lon", "lev")]
     sizes = [lax.axis_size(axis) for axis in ("lat", "lon", "lev")]
     has = [(at > 0, at < size - 1) for at, size in zip(place, sizes)]
@@ -33,6 +33,16 @@
         for axis, at in zip(("lat", "lon", "lev"), place)
     ]
 
+    barrier = pltpu.get_barrier_semaphore()
+    count = 0
+    for axis in (2, 1, 0):
+        for side in range(2):
+            count = count + has[axis][side].astype(jnp.int32)
+
+            @pl.when(has[axis][side])
+            def _():
+                pl.semaphore_signal(barrier, inc=1, device_id=towards[axis][side], device_id_type=MESH)
+
     spans = [(plane, 1, at, size) for at, size in pieces[0] for plane in (0, planes - 1)]
     spans.append((1, planes - 2, 0, rows))
     loads = [
@@ -45,25 +55,25 @@
     ]
     loads.append(pltpu.make_async_copy(earlier_ref, field.at[1, :, pl.ds(1, rows)], load_sem.at[5]))
     loads.append(pltpu.make_async_copy(speed_ref, speed, load_sem.at[6]))
+    loads += [
+        pltpu.make_async_copy(
+            speed_ref.at[(planes - 1) * side, pl.ds(begin, rows - begin)], face_speed_ref.at[side], load_sem.at[7 + side]
+        )
+        for side in range(2)
+    ]
     for load in loads:
         load.start()
 
-    barrier = pltpu.get_barrier_semaphore()
-    count = 0
-    for axis in range(3):
-        for side in range(2):
-            count = count + has[axis][side].astype(jnp.int32)
-
-            @pl.when(has[axis][side])
-            def _():
-                pl.semaphore_signal(barrier, inc=1, device_id=towards[axis][side], device_id_type=MESH)
-
     pl.semaphore_wait(barrier, count)
 
     def copy_j(step, piece, side):
         at, size = pieces[step][piece]
+        if step == STEPS - 1 and at >= begin:
+            source = face_ref.at[side, pl.ds(at - begin, size)]
+        else:
+            source = field.at[step % 2, (planes - 1) * side, pl.ds(at + 1, size)]
         return pltpu.make_async_remote_copy(
-            src_ref=field.at[step % 2, (planes - 1) * side, pl.ds(at + 1, size)],
+            src_ref=source,
             dst_ref=halo_j.at[step, 1 - side, pl.ds(at, size)],
             send_sem=send_j.at[step, side, piece],
             recv_sem=recv_j.at[step, 1 - side, piece],
@@ -154,7 +164,8 @@
             body(index)
             return 0
 
-        lax.fori_loop(0, count, one, 0)
+        if count:
+            lax.fori_loop(0, count, one, 0)
 
     for piece in range(len(pieces[0])):
         loads[2 * piece].wait()
@@ -185,30 +196,45 @@
     pack(0)
     send_sides(0)
     loads[5].wait()
-    loads[6].wait()
+    for load in loads[6:]:
+        load.wait()
 
     level = lax.broadcasted_iota(jnp.int32, (depth, 128), 0)
     first, last = level == 0, level == depth - 1
 
-    def compute_row(step, i, some):
+    def compute_row(step, i, to_face=False):
         old, new = step % 2, (step + 1) % 2
         slots = [jnp.where(has[0][side], step, 0) for side in range(2)]
-        for plane in some:
+        for plane in range(planes):
             here = field[old, plane, i + 1]
-            below = halo_j[slots[0], 0, i] if plane == 0 else field[old, plane - 1, i + 1]
-            above = halo_j[slots[1], 1, i] if plane == planes - 1 else field[old, plane + 1, i + 1]
-            spread = below + above + field[old, plane, i] + field[old, plane, i + 2]
-            k_low = jnp.where(first, halo_k[step, 0, plane, pl.ds(i, 1), :], pltpu.roll(here, 1, 0))
-            k_high = jnp.where(last, halo_k[step, 1, plane, pl.ds(i, 1), :], pltpu.roll(here, depth - 1, 0))
-            spread = spread + k_low + k_high - 6.0 * here
+            terms = []
+            if plane > 0:
+                terms.append(field[old, plane - 1, i + 1])
+            elif step < STEPS - 1:
+                terms.append(halo_j[slots[0], 0, i])
+            if plane < planes - 1:
+                terms.append(field[old, plane + 1, i + 1])
+            elif step < STEPS - 1:
+                terms.append(halo_j[slots[1], 1, i])
+            terms += [field[old, plane, i], field[old, plane, i + 2]]
+            terms.append(jnp.where(first, halo_k[step, 0, plane, pl.ds(i, 1), :], pltpu.roll(here, 1, 0)))
+            terms.append(jnp.where(last, halo_k[step, 1, plane, pl.ds(i, 1), :], pltpu.roll(here, depth - 1, 0)))
+            spread = functools.reduce(jnp.add, terms) - 6.0 * here
             later = 2.0 * here - field[new, plane, i + 1] + speed[plane, i] * spread
             if step < STEPS - 1:
                 field[new, plane, i + 1] = later
+                if to_face and plane in (0, planes - 1):
+                    face_ref[plane // (planes - 1), i - begin] = later
+            elif plane in (0, planes - 1):
+                outer_ref[plane // (planes - 1), i] = later
             else:
-                out_ref[plane, i] = later
-
-    def compute(step, at, size, some):
-        each(size, lambda i: compute_row(step, at + i, some))
+                inner_ref[plane - 1, i] = later
+
+    def add_halo(step, i):
+        for side in range(2):
+            plane = (planes - 1) * side
+            slot = jnp.where(has[0][side], step, 0)
+            outer_ref[side, i] = outer_ref[side, i] + speed[plane, i] * halo_j[slot, side, i]
 
     for step in range(STEPS - 1):
         wait_sides(step)
@@ -219,72 +245,224 @@
             if step > 0:
                 wait_piece_sent(step - 1, piece)
             wait_piece(step, piece)
-            compute(step, at, size, range(planes))
+            kept = min(max(begin - at, 0), size) if step == STEPS - 2 else size
+            each(kept, lambda i: compute_row(step, at + i))
+            each(size - kept, lambda i: compute_row(step, at + kept + i, True))
             while sent < len(pieces[step + 1]) and sum(pieces[step + 1][sent]) <= at + size:
-                send_piece(step + 1, sent)
+                if step + 1 < STEPS - 1:
+                    send_piece(step + 1, sent)
+                else:
+                    @pl.when(is_early(place[1], sent))
+                    def _():
+                        send_piece(step + 1, sent)
+
                 sent += 1
         pack(step + 1)
         send_sides(step + 1)
 
     step = STEPS - 1
     wait_sides(step)
-    compute(step, 0, rows, range(1, planes - 1))
-    for piece, (at, size) in enumerate(pieces[step]):
-        wait_piece(step, piece)
-        compute(step, at, size, (0, planes - 1))
+    each(rows, lambda i: compute_row(step, i))
+    for piece in range(len(pieces[step - 1])):
+        wait_piece_sent(step - 1, piece)
     for before in (step - 1, step):
         wait_sides_sent(before)
-        for piece in range(len(pieces[before])):
-            wait_piece_sent(before, piece)
-
-
-def write_out(value_ref, out_ref, sem):
-    rows = value_ref.shape[1]
+    for piece, (at, size) in enumerate(pieces[step]):
+        @pl.when(is_early(place[1], piece))
+        def _():
+            wait_piece(step, piece)
+            each(size, lambda i: add_halo(step, at + i))
+            wait_piece_sent(step, piece)
+
+
+def is_early(lon, piece):
+    return jnp.where(lon % 2 == 0, EARLY[0], EARLY[1]) > piece
+
+
+def rest_kernel(rows, outer_ref, face_ref, face_speed_ref, token_ref, rest_ref, halo, send, recv):
+    del token_ref
+    depth = face_ref.shape[2]
+    pieces = cuts(STEPS - 1, rows)
+    begin = pieces[min(EARLY)][0]
+    at_lat, at_lon = lax.axis_index("lat"), lax.axis_index("lon")
+    has = (at_lat > 0, at_lat < lax.axis_size("lat") - 1)
+    towards = ({"lat": at_lat - 1}, {"lat": at_lat + 1})
+
+    barrier = pltpu.get_barrier_semaphore()
+    for side in range(2):
+        @pl.when(has[side])
+        def _():
+            pl.semaphore_signal(barrier, inc=1, device_id=towards[side], device_id_type=MESH)
+
+    pl.semaphore_wait(barrier, has[0].astype(jnp.int32) + has[1].astype(jnp.int32))
+
+    def copy(piece, side):
+        at, size = pieces[piece]
+        return pltpu.make_async_remote_copy(
+            src_ref=face_ref.at[side, pl.ds(at - begin, size)],
+            dst_ref=halo.at[1 - side, pl.ds(at - begin, size)],
+            send_sem=send.at[side, piece],
+            recv_sem=recv.at[1 - side, piece],
+            device_id=towards[side],
+            device_id_type=MESH,
+        )
+
+    late = range(min(EARLY), len(pieces))
+    for piece in late:
+        for side in range(2):
+            @pl.when(has[side] & jnp.logical_not(is_early(at_lon, piece)))
+            def _():
+                copy(piece, side).start()
+
+    for side in range(2):
+        @pl.when(jnp.logical_not(has[side]))
+        def _():
+            def row(i, _):
+                halo[side, i] = jnp.zeros((depth, 128), jnp.float32)
+                return 0
+
+            lax.fori_loop(0, rows - begin, row, 0)
+
+    for piece in late:
+        at, size = pieces[piece]
+
+        @pl.when(jnp.logical_not(is_early(at_lon, piece)))
+        def _():
+            for side in range(2):
+                @pl.when(has[1 - side])
+                def _():
+                    copy(piece, side).wait_recv()
+
+            def row(i, _):
+                for side in range(2):
+                    on = at - begin + i
+                    rest_ref[side, on] = outer_ref[side, at + i] + face_speed_ref[side, on] * halo[side, on]
+                return 0
+
+            lax.fori_loop(0, size, row, 0)
+
+    for piece in late:
+        for side in range(2):
+            @pl.when(has[side] & jnp.logical_not(is_early(at_lon, piece)))
+            def _():
+                copy(piece, side).wait_send()
+
+
+def run(copies):
+    for condition, copy in copies:
+        @pl.when(condition)
+        def _():
+            copy.start()
+
+    for condition, copy in copies:
+        @pl.when(condition)
+        def _():
+            copy.wait()
+
+
+def write_early(inner_ref, outer_ref, out_ref, token_ref, sem):
+    planes, rows = out_ref.shape[:2]
+    lon = lax.axis_index("lon")
     copies = [
-        pltpu.make_async_copy(value_ref.at[:, pl.ds(at, OUT)], out_ref.at[:, pl.ds(at, OUT)], sem.at[at // OUT])
-        for at in range(0, rows, OUT)
+        (lon >= 0, pltpu.make_async_copy(inner_ref.at[plane], out_ref.at[plane + 1], sem.at[plane]))
+        for plane in range(planes - 2)
     ]
-    for copy in copies:
-        copy.start()
-    for copy in copies:
-        copy.wait()
+    for piece, (at, size) in enumerate(cuts(STEPS - 1, rows)[:max(EARLY)]):
+        for side in range(2):
+            copies.append((is_early(lon, piece), pltpu.make_async_copy(
+                outer_ref.at[side, pl.ds(at, size)],
+                out_ref.at[(planes - 1) * side, pl.ds(at, size)],
+                sem.at[len(copies)],
+            )))
+    run(copies)
+    token_ref[...] = jnp.zeros_like(token_ref)
+
+
+def write_rest(rest_ref, begun_ref, out_ref, sem):
+    del begun_ref
+    planes, rows = out_ref.shape[:2]
+    lon = lax.axis_index("lon")
+    pieces = cuts(STEPS - 1, rows)
+    begin = pieces[min(EARLY)][0]
+    spans = [
+        (side, at, size, jnp.logical_not(is_early(lon, piece)))
+        for piece, (at, size) in enumerate(pieces) if piece >= min(EARLY) for side in range(2)
+    ]
+    run([
+        (condition, pltpu.make_async_copy(
+            rest_ref.at[side, pl.ds(at - begin, size)],
+            out_ref.at[(planes - 1) * side, pl.ds(at, size)],
+            sem.at[index]))
+        for index, (side, at, size, condition) in enumerate(spans)
+    ])
 
 
 def local(field_now, earlier, speed_square):
     planes, rows, depth, members = field_now.shape
-    f32 = jnp.float32
-    any_spec = pl.BlockSpec(memory_space=pl.ANY)
-    later = pl.pallas_call(
+    shape, f32 = field_now.shape, jnp.float32
+    begin = cuts(STEPS - 1, rows)[min(EARLY)][0]
+    most = max(map(len, PIECES))
+    in_hbm, in_vmem = pl.BlockSpec(memory_space=pl.ANY), pl.BlockSpec(memory_space=pltpu.VMEM)
+    dma = pltpu.SemaphoreType.DMA
+    inner, outer, face, face_speed = pl.pallas_call(
         kernel,
-        out_shape=pltpu.VMEM(field_now.shape, f32),
-        in_specs=[any_spec] * 3,
-        out_specs=pl.BlockSpec(memory_space=pltpu.VMEM),
+        out_shape=(
+            pltpu.VMEM((planes - 2, rows, depth, members), f32),
+            pltpu.VMEM((2, rows, depth, members), f32),
+            pltpu.VMEM((2, rows - begin, depth, members), f32),
+            pltpu.VMEM((2, rows - begin, depth, members), f32),
+        ),
+        in_specs=[in_hbm] * 3,
+        out_specs=(in_vmem,) * 4,
         scratch_shapes=[
             pltpu.VMEM((2, planes, rows + 2, depth, members), f32),
-            pltpu.VMEM((planes, rows, depth, members), f32),
+            pltpu.VMEM(shape, f32),
             pltpu.VMEM((STEPS, 2, rows, depth, members), f32),
             pltpu.VMEM((STEPS, 2, planes, rows, members), f32),
             pltpu.VMEM((STEPS, 2, planes, rows, members), f32),
-            pltpu.SemaphoreType.DMA((7,)),
-            pltpu.SemaphoreType.DMA((STEPS, 2, max(map(len, PIECES)))),
-            pltpu.SemaphoreType.DMA((STEPS, 2, max(map(len, PIECES)))),
-            pltpu.SemaphoreType.DMA((STEPS, 2)),
-            pltpu.SemaphoreType.DMA((STEPS, 2)),
-            pltpu.SemaphoreType.DMA((STEPS, 2)),
-            pltpu.SemaphoreType.DMA((STEPS, 2)),
+            dma((9,)),
+            dma((STEPS, 2, most)),
+            dma((STEPS, 2, most)),
+            dma((STEPS, 2)),
+            dma((STEPS, 2)),
+            dma((STEPS, 2)),
+            dma((STEPS, 2)),
         ],
         compiler_params=pltpu.CompilerParams(
             collective_id=0, has_side_effects=True, vmem_limit_bytes=46 * 2**20
         ),
     )(field_now, earlier, speed_square)
+    begun, token = pl.pallas_call(
+        write_early,
+        out_shape=(jax.ShapeDtypeStruct(shape, f32), pltpu.VMEM((8, 128), f32)),
+        in_specs=[in_vmem] * 2,
+        out_specs=(in_hbm, in_vmem),
+        scratch_shapes=[dma((planes - 2 + 2 * max(EARLY),))],
+        compiler_params=pltpu.CompilerParams(vmem_limit_bytes=2**20),
+    )(inner, outer)
+    rest = pl.pallas_call(
+        functools.partial(rest_kernel, rows),
+        out_shape=pltpu.VMEM((2, rows - begin, depth, members), f32),
+        in_specs=[in_vmem] * 4,
+        out_specs=in_vmem,
+        scratch_shapes=[
+            pltpu.VMEM((2, rows - begin, depth, members), f32),
+            dma((2, most)),
+            dma((2, most)),
+        ],
+        compiler_params=pltpu.CompilerParams(
+            collective_id=1, has_side_effects=True, vmem_limit_bytes=8 * 2**20
+        ),
+    )(outer, face, face_speed, token)
     return pl.pallas_call(
-        write_out,
-        out_shape=jax.ShapeDtypeStruct(field_now.shape, f32),
-        in_specs=[pl.BlockSpec(memory_space=pltpu.VMEM)],
-        out_specs=any_spec,
-        scratch_shapes=[pltpu.SemaphoreType.DMA((rows // OUT,))],
+        write_rest,
+        out_shape=jax.ShapeDtypeStruct(shape, f32),
+        in_specs=[in_vmem, in_hbm],
+        out_specs=in_hbm,
+        input_output_aliases={1: 0},
+        scratch_shapes=[dma((2 * most,))],
         compiler_params=pltpu.CompilerParams(vmem_limit_bytes=2**20),
-    )(later)
+    )(rest, begun)
 
 
 def solution(mesh):

time: 190 us -> 187 us (0.984)
  Pallas kernels: 190 us -> 187 us
    pallas_call x2 -> x4, Pallas kernels: 190 us -> 187 us  [the longest x1 173 us: local(): pl.pallas_call(kernel, out_shape=(pltpu.VMEM((planes - 2, rows, depth, me...]
where the time goes in v4:
time: 187 us
  Pallas kernels  187 us (100%)
    pallas_call x1, Pallas kernels, local(): pl.pallas_call(kernel, out_shape=(pltpu.VMEM((planes - 2, rows, depth, me...  173 us
    pallas_call x1, Pallas kernels, local(): pl.pallas_call(functools.partial(rest_kernel, rows), out_shape=pltpu.VMEM...  9.98 us

profile of v4, /device:TPU:1, one launch (start us, length us, event | category | flops | bytes accessed | tf_op | source)
XLA Modules:
  0.0 187.1 jit_solution(2029632759204476916)
XLA Ops:
  0.0 173.0 %shard_map.37 = (f32[2,64,64,128]{3,2,1,0:T(8,128)S(1)}, f32[2,64,64,128]{3,2,1,0:T(8,128)S(1)}, f32[2,36,64,128]{3,2,1,0:T(8,128)S(1)}, f32[2,36,64,128]{3,2,1,0:T(8,128)S(1)}) custom-call(f32[4,64,64,128]{3,2,1,0:T(8,128)} %now_ref.1, f32[4,64,64,128]{3,2,1,0:T(8,128)} %earlier_ref.1, f32[4,64,64,128]{3,2,1,0:T(8,128)} %speed_ref.1), custom_call_target="tpu_custom_call" | custom-call | tf_op jit(solution)/shard_map/pallas_call | solution.py:407
  173.1 3.2 %shard_map.38 = (f32[4,64,64,128]{3,2,1,0:T(8,128)}, f32[8,128]{1,0:T(8,128)S(1)}) custom-call(f32[2,64,64,128]{3,2,1,0:T(8,128)S(1)} %get-tuple-element.14.inner_ref, f32[2,64,64,128]{3,2,1,0:T(8,128)S(1)} %get-tuple-element.11.outer_ref), custom_call_target="tpu_custom_call" | custom-call | tf_op jit(solution)/shard_map/pallas_call | solution.py:435
  176.3 10.0 %shard_map.39.rest_ref = f32[2,36,64,128]{3,2,1,0:T(8,128)S(1)} custom-call(f32[2,64,64,128]{3,2,1,0:T(8,128)S(1)} %get-tuple-element.11.outer_ref, f32[2,36,64,128]{3,2,1,0:T(8,128)S(1)} %get-tuple-element.12.face_ref, f32[2,36,64,128]{3,2,1,0:T(8,128)S(1)} %get-tuple-element.13.face_speed_ref, f32[8,128]{1,0:T(8,128)S(1)} %get-tuple-element.15.token_ref), custom_call_target="tpu_custom_call" | custom-call | tf_op jit(solution)/shard_map/pallas_call | solution.py:443
  186.3 0.8 shard_map.40

commit v5 on v4

--- a/solution.py
+++ b/solution.py
@@ -20,7 +20,7 @@
 
 def kernel(
     now_ref, earlier_ref, speed_ref, inner_ref, outer_ref, face_ref, face_speed_ref, field, speed, halo_j, halo_k, pack_k,
-    load_sem, send_j, recv_j, send_i, recv_i, send_k, recv_k,
+    met_sem, load_sem, send_j, recv_j, send_i, recv_i, send_k, recv_k,
 ):
     planes, rows, depth, _ = now_ref.shape
     pieces = [cuts(step, rows) for step in range(STEPS)]
@@ -33,15 +33,29 @@
         for axis, at in zip(("lat", "lon", "lev"), place)
     ]
 
+    lat, lon, lev = place
+    x_lo, x_hi = lon // 2, lev % 2
+    beside = [
+        (x_lo + x_hi > 0, {"lon": lon + 2 - 4 * x_lo, "lev": lev - 1 + x_lo}),
+        (x_lo + x_hi < 2, {"lon": lon + 2 - 4 * x_lo, "lev": lev + x_lo}),
+        (lev >= 2, {"lev": lev - 2}),
+        (lev < sizes[2] - 2, {"lev": lev + 2}),
+        (lon >= 0, {"lon": lon + 1 - 2 * (lon % 2)}),
+    ]
+
+    def greet(semaphore, devices):
+        count = 0
+        for there, device in devices:
+            count = count + there.astype(jnp.int32)
+
+            @pl.when(there)
+            def _():
+                pl.semaphore_signal(semaphore, inc=1, device_id=device, device_id_type=MESH)
+
+        return count
+
     barrier = pltpu.get_barrier_semaphore()
-    count = 0
-    for axis in (2, 1, 0):
-        for side in range(2):
-            count = count + has[axis][side].astype(jnp.int32)
-
-            @pl.when(has[axis][side])
-            def _():
-                pl.semaphore_signal(barrier, inc=1, device_id=towards[axis][side], device_id_type=MESH)
+    count = greet(barrier, beside + [(has[0][side], towards[0][side]) for side in range(2)])
 
     spans = [(plane, 1, at, size) for at, size in pieces[0] for plane in (0, planes - 1)]
     spans.append((1, planes - 2, 0, rows))
@@ -171,6 +185,9 @@
         loads[2 * piece].wait()
         loads[2 * piece + 1].wait()
         send_piece(0, piece)
+
+    for index in range(2):
+        pl.semaphore_wait(met_sem.at[index], greet(met_sem.at[index], beside))
 
     for side in range(2):
         @pl.when(jnp.logical_not(has[1][side]))
@@ -420,6 +437,7 @@
             pltpu.VMEM((STEPS, 2, rows, depth, members), f32),
             pltpu.VMEM((STEPS, 2, planes, rows, members), f32),
             pltpu.VMEM((STEPS, 2, planes, rows, members), f32),
+            pltpu.SemaphoreType.REGULAR((2,)),
             dma((9,)),
             dma((STEPS, 2, most)),
             dma((STEPS, 2, most)),

time: 187 us -> 186 us (level)
  no operation moved by 1% of the time
where the time goes in v5:
time: 186 us
  Pallas kernels  186 us (100%)
    pallas_call x1, Pallas kernels, local(): pl.pallas_call(kernel, out_shape=(pltpu.VMEM((planes - 2, rows, depth, me...  172 us
    pallas_call x1, Pallas kernels, local(): pl.pallas_call(functools.partial(rest_kernel, rows), out_shape=pltpu.VMEM...  9.5 us

profile of v5, /device:TPU:1, one launch (start us, length us, event | category | flops | bytes accessed | tf_op | source)
XLA Modules:
  0.0 185.9 jit_solution(12553668832562127516)
XLA Ops:
  0.0 172.3 %shard_map.37 = (f32[2,64,64,128]{3,2,1,0:T(8,128)S(1)}, f32[2,64,64,128]{3,2,1,0:T(8,128)S(1)}, f32[2,36,64,128]{3,2,1,0:T(8,128)S(1)}, f32[2,36,64,128]{3,2,1,0:T(8,128)S(1)}) custom-call(f32[4,64,64,128]{3,2,1,0:T(8,128)} %now_ref.1, f32[4,64,64,128]{3,2,1,0:T(8,128)} %earlier_ref.1, f32[4,64,64,128]{3,2,1,0:T(8,128)} %speed_ref.1), custom_call_target="tpu_custom_call" | custom-call | tf_op jit(solution)/shard_map/pallas_call | solution.py:424
  172.3 3.2 %shard_map.38 = (f32[4,64,64,128]{3,2,1,0:T(8,128)}, f32[8,128]{1,0:T(8,128)S(1)}) custom-call(f32[2,64,64,128]{3,2,1,0:T(8,128)S(1)} %get-tuple-element.14.inner_ref, f32[2,64,64,128]{3,2,1,0:T(8,128)S(1)} %get-tuple-element.11.outer_ref), custom_call_target="tpu_custom_call" | custom-call | tf_op jit(solution)/shard_map/pallas_call | solution.py:453
  175.5 9.5 %shard_map.39.rest_ref = f32[2,36,64,128]{3,2,1,0:T(8,128)S(1)} custom-call(f32[2,64,64,128]{3,2,1,0:T(8,128)S(1)} %get-tuple-element.11.outer_ref, f32[2,36,64,128]{3,2,1,0:T(8,128)S(1)} %get-tuple-element.12.face_ref, f32[2,36,64,128]{3,2,1,0:T(8,128)S(1)} %get-tuple-element.13.face_speed_ref, f32[8,128]{1,0:T(8,128)S(1)} %get-tuple-element.15.token_ref), custom_call_target="tpu_custom_call" | custom-call | tf_op jit(solution)/shard_map/pallas_call | solution.py:461
  185.0 0.8 shard_map.40

commit v6 on v5

--- a/solution.py
+++ b/solution.py
@@ -57,6 +57,7 @@
     barrier = pltpu.get_barrier_semaphore()
     count = greet(barrier, beside + [(has[0][side], towards[0][side]) for side in range(2)])
 
+    faces = 2 * len(pieces[0])
     spans = [(plane, 1, at, size) for at, size in pieces[0] for plane in (0, planes - 1)]
     spans.append((1, planes - 2, 0, rows))
     loads = [
@@ -67,15 +68,15 @@
         )
         for index, (plane, count, at, size) in enumerate(spans)
     ]
-    loads.append(pltpu.make_async_copy(earlier_ref, field.at[1, :, pl.ds(1, rows)], load_sem.at[5]))
-    loads.append(pltpu.make_async_copy(speed_ref, speed, load_sem.at[6]))
+    loads.append(pltpu.make_async_copy(earlier_ref, field.at[1, :, pl.ds(1, rows)], load_sem.at[faces + 1]))
+    loads.append(pltpu.make_async_copy(speed_ref, speed, load_sem.at[faces + 2]))
     loads += [
         pltpu.make_async_copy(
-            speed_ref.at[(planes - 1) * side, pl.ds(begin, rows - begin)], face_speed_ref.at[side], load_sem.at[7 + side]
+            speed_ref.at[(planes - 1) * side, pl.ds(begin, rows - begin)], face_speed_ref.at[side], load_sem.at[faces + 3 + side]
         )
         for side in range(2)
     ]
-    for load in loads:
+    for load in loads[:faces]:
         load.start()
 
     pl.semaphore_wait(barrier, count)
@@ -186,6 +187,9 @@
         loads[2 * piece + 1].wait()
         send_piece(0, piece)
 
+    for load in loads[faces:]:
+        load.start()
+
     for index in range(2):
         pl.semaphore_wait(met_sem.at[index], greet(met_sem.at[index], beside))
 
@@ -209,11 +213,10 @@
 
             lax.fori_loop(0, rows, row, 0)
 
-    loads[4].wait()
+    loads[faces].wait()
     pack(0)
     send_sides(0)
-    loads[5].wait()
-    for load in loads[6:]:
+    for load in loads[faces + 1:]:
         load.wait()
 
     level = lax.broadcasted_iota(jnp.int32, (depth, 128), 0)
@@ -257,10 +260,11 @@
         wait_sides(step)
         if step > 0:
             wait_sides_sent(step - 1)
-        sent = 0
+        sent = free = 0
         for piece, (at, size) in enumerate(pieces[step]):
-            if step > 0:
-                wait_piece_sent(step - 1, piece)
+            while step > 0 and free < len(pieces[step - 1]) and pieces[step - 1][free][0] < at + size:
+                wait_piece_sent(step - 1, free)
+                free += 1
             wait_piece(step, piece)
             kept = min(max(begin - at, 0), size) if step == STEPS - 2 else size
             each(kept, lambda i: compute_row(step, at + i))
@@ -438,7 +442,7 @@
             pltpu.VMEM((STEPS, 2, planes, rows, members), f32),
             pltpu.VMEM((STEPS, 2, planes, rows, members), f32),
             pltpu.SemaphoreType.REGULAR((2,)),
-            dma((9,)),
+            dma((2 * len(PIECES[0]) + 5,)),
             dma((STEPS, 2, most)),
             dma((STEPS, 2, most)),
             dma((STEPS, 2)),

time: 186 us -> 186 us (level)
  no operation moved by 1% of the time
where the time goes in v6:
time: 186 us
  Pallas kernels  186 us (100%)
    pallas_call x1, Pallas kernels, local(): pl.pallas_call(kernel, out_shape=(pltpu.VMEM((planes - 2, rows, depth, me...  172 us
    pallas_call x1, Pallas kernels, local(): pl.pallas_call(functools.partial(rest_kernel, rows), out_shape=pltpu.VMEM...  9.5 us

profile of v6, /device:TPU:1, one launch (start us, length us, event | category | flops | bytes accessed | tf_op | source)
XLA Modules:
  0.0 185.9 jit_solution(10558300936274803132)
XLA Ops:
  0.0 172.3 %shard_map.37 = (f32[2,64,64,128]{3,2,1,0:T(8,128)S(1)}, f32[2,64,64,128]{3,2,1,0:T(8,128)S(1)}, f32[2,36,64,128]{3,2,1,0:T(8,128)S(1)}, f32[2,36,64,128]{3,2,1,0:T(8,128)S(1)}) custom-call(f32[4,64,64,128]{3,2,1,0:T(8,128)} %now_ref.1, f32[4,64,64,128]{3,2,1,0:T(8,128)} %earlier_ref.1, f32[4,64,64,128]{3,2,1,0:T(8,128)} %speed_ref.1), custom_call_target="tpu_custom_call" | custom-call | tf_op jit(solution)/shard_map/pallas_call | solution.py:428
  172.3 3.2 %shard_map.38 = (f32[4,64,64,128]{3,2,1,0:T(8,128)}, f32[8,128]{1,0:T(8,128)S(1)}) custom-call(f32[2,64,64,128]{3,2,1,0:T(8,128)S(1)} %get-tuple-element.14.inner_ref, f32[2,64,64,128]{3,2,1,0:T(8,128)S(1)} %get-tuple-element.11.outer_ref), custom_call_target="tpu_custom_call" | custom-call | tf_op jit(solution)/shard_map/pallas_call | solution.py:457
  175.5 9.5 %shard_map.39.rest_ref = f32[2,36,64,128]{3,2,1,0:T(8,128)S(1)} custom-call(f32[2,64,64,128]{3,2,1,0:T(8,128)S(1)} %get-tuple-element.11.outer_ref, f32[2,36,64,128]{3,2,1,0:T(8,128)S(1)} %get-tuple-element.12.face_ref, f32[2,36,64,128]{3,2,1,0:T(8,128)S(1)} %get-tuple-element.13.face_speed_ref, f32[8,128]{1,0:T(8,128)S(1)} %get-tuple-element.15.token_ref), custom_call_target="tpu_custom_call" | custom-call | tf_op jit(solution)/shard_map/pallas_call | solution.py:465
  185.0 0.8 shard_map.40

commit v7 on v6

--- a/solution.py
+++ b/solution.py
@@ -314,6 +314,10 @@
         @pl.when(has[side])
         def _():
             pl.semaphore_signal(barrier, inc=1, device_id=towards[side], device_id_type=MESH)
+
+    @pl.when(at_lon % 2 == 1)
+    def _():
+        pl.delay(2000)
 
     pl.semaphore_wait(barrier, has[0].astype(jnp.int32) + has[1].astype(jnp.int32))
 

time: 186 us -> 186 us (level)
  no operation moved by 1% of the time
where the time goes in v7:
time: 186 us
  Pallas kernels  186 us (100%)
    pallas_call x1, Pallas kernels, local(): pl.pallas_call(kernel, out_shape=(pltpu.VMEM((planes - 2, rows, depth, me...  172 us
    pallas_call x1, Pallas kernels, local(): pl.pallas_call(functools.partial(rest_kernel, rows), out_shape=pltpu.VMEM...  9.47 us

profile of v7, /device:TPU:1, one launch (start us, length us, event | category | flops | bytes accessed | tf_op | source)
XLA Modules:
  0.0 185.8 jit_solution(2803887388624021265)
XLA Ops:
  0.0 172.3 %shard_map.37 = (f32[2,64,64,128]{3,2,1,0:T(8,128)S(1)}, f32[2,64,64,128]{3,2,1,0:T(8,128)S(1)}, f32[2,36,64,128]{3,2,1,0:T(8,128)S(1)}, f32[2,36,64,128]{3,2,1,0:T(8,128)S(1)}) custom-call(f32[4,64,64,128]{3,2,1,0:T(8,128)} %now_ref.1, f32[4,64,64,128]{3,2,1,0:T(8,128)} %earlier_ref.1, f32[4,64,64,128]{3,2,1,0:T(8,128)} %speed_ref.1), custom_call_target="tpu_custom_call" | custom-call | tf_op jit(solution)/shard_map/pallas_call | solution.py:432
  172.3 3.2 %shard_map.38 = (f32[4,64,64,128]{3,2,1,0:T(8,128)}, f32[8,128]{1,0:T(8,128)S(1)}) custom-call(f32[2,64,64,128]{3,2,1,0:T(8,128)S(1)} %get-tuple-element.14.inner_ref, f32[2,64,64,128]{3,2,1,0:T(8,128)S(1)} %get-tuple-element.11.outer_ref), custom_call_target="tpu_custom_call" | custom-call | tf_op jit(solution)/shard_map/pallas_call | solution.py:461
  175.5 9.5 %shard_map.39.rest_ref = f32[2,36,64,128]{3,2,1,0:T(8,128)S(1)} custom-call(f32[2,64,64,128]{3,2,1,0:T(8,128)S(1)} %get-tuple-element.11.outer_ref, f32[2,36,64,128]{3,2,1,0:T(8,128)S(1)} %get-tuple-element.12.face_ref, f32[2,36,64,128]{3,2,1,0:T(8,128)S(1)} %get-tuple-element.13.face_speed_ref, f32[8,128]{1,0:T(8,128)S(1)} %get-tuple-element.15.token_ref), custom_call_target="tpu_custom_call" | custom-call | tf_op jit(solution)/shard_map/pallas_call | solution.py:469
  185.0 0.8 shard_map.40
